TPU v7x, 512 devices: a whole 4x8x8 slice. The times are simulated.
512 devices in a mesh: cx: 16 (over z_hi, y), cy: 32 (over x, z_lo, core).
Axes of the slice: x: 4, y: 8, z: 8 (z_hi: 2, z_lo: 4; z = z_hi * 4 + z_lo), core: 2. Of those that a mesh axis runs over, the one named last changes fastest.
Arguments:
- queries: bfloat16 [7, 32768, 128], P(None, ('cx', 'cy')), may hold values from -8 to 8, as said below
- keys: bfloat16 [32768, 128], P(('cx', 'cy')), may hold values from -40 to 40, as said below
- values: bfloat16 [32768, 128], P(('cx', 'cy')), may hold values from -6 to 6
Outputs:
- attended: bfloat16 [7, 32768, 128], P(None, ('cx', 'cy'))
Inputs may be any that keep to these rules, and one draw needn't show every extreme that they name: `queries`: every query is noise of about unit size in each entry plus one common direction of length 4, the same for all heads and tokens. The keys of the first four prompt positions carry a large component along the queries' common direction, so they draw much of every query's attention; all other keys are noise of about unit size in each entry.
All inputs are finite; a program needn't handle non-finite values.
Results may differ from a plain program's by a relative error of at most 0.001.
Values may be sent and summed in bfloat16 or wider, within the bound.
No kernel may reach another device: no remote copies, remote signals or barrier semaphores. Data moves between devices by JAX's collectives and lax.ppermute only.
A program may use at most 192 MiB of HBM per device.

v0:
```python
import functools
import math

import jax
import jax.numpy as jnp
from jax import lax
from jax.experimental import pallas as pl
from jax.experimental.pallas import tpu as pltpu
from jax.sharding import Mesh
from jax.sharding import PartitionSpec as P


AXES = ("zh", "y", "x", "zl", "c")
SIZES = (2, 8, 4, 4, 2)
TEAM = ("x", "c")
Z = ("zh", "zl")

HEAD = 128
GROUP = 7
TOK = 64
ROWS = GROUP * TOK
MATES = 8
HOPS = (0, 3, 1, 2)
SEQ = 32768
SINKS = 4
ALL_ROWS = MATES * ROWS
CHUNKS = 4
STAT = ROWS
EXTRA = STAT + 16
PAYLOAD = EXTRA + 16
masked = -(2.0**100)
SCALE = HEAD**-0.5 * math.log2(math.e)
f32 = jnp.float32
bf16 = jnp.bfloat16


def place():
    return tuple(lax.axis_index(name) for name in AXES)


def rows_of(mate):
    if isinstance(mate, int):
        return slice(mate * ROWS, (mate + 1) * ROWS)
    return pl.ds(pl.multiple_of(mate * ROWS, ROWS), ROWS)


def queries_of(q_refs, mate):
    return q_refs[mate // 2][rows_of(mate % 2), :]


def scores_of(q, k):
    return lax.dot_general(q, k, (((1,), (1,)), ((), ())), preferred_element_type=f32) * SCALE


def number_of(at, mate):
    hop = HOPS[mate // 2] if isinstance(mate, int) else jnp.where(mate < 2, 0, jnp.where(mate < 4, 3, jnp.where(mate < 6, 1, 2)))
    return (at[2] + hop) % 4 * 2 + mate % 2


def positions(at, zk, ys, lane, count):
    key = lax.broadcasted_iota(jnp.int32, (1, count), 1)
    block = ((zk // 4) * 8 + ys + (key >> 6)) * 32 + at[2] * 8 + (zk % 4) * 2 + lane
    return block * TOK + (key & (TOK - 1))


def query_positions(at, mate):
    zh, y, _, zl, _ = at
    number = number_of(at, mate)
    block = (zh * 8 + y) * 32 + (number // 2) * 8 + zl * 2 + number % 2
    return block * TOK + lax.broadcasted_iota(jnp.int32, (TOK, 1), 0)


def keep(visible, array, other):
    array = array.reshape(GROUP, TOK, visible.shape[1])
    return jnp.where(visible[None], array, other).reshape(ROWS, visible.shape[1])


def mix(weights, v):
    return jnp.dot(weights.astype(bf16), v, preferred_element_type=f32)


def with_ones(at, v, zk, ys, lane):
    rows = v.shape[0]
    start = ((zk * 8 + ys) * 4 + at[2]) * 2 + lane
    row = lax.broadcasted_iota(jnp.int32, (rows, 1), 0)
    v = jnp.concatenate([v, jnp.ones((rows, HEAD), bf16)], axis=1)
    return jnp.where((start > 0) | (row >= SINKS), v.astype(f32), 0.0).astype(bf16)


def keys_at(ref, lane, ys):
    return ref[lane, pl.ds(ys, 4), :, :HEAD].reshape(256, HEAD)


def values_at(ref, lane, ys):
    return ref[lane, pl.ds(ys, 4), :, HEAD:].reshape(256, HEAD)


def fold_part(at, q_refs, sum_ref, kv_ref, zk, ys, lane):
    k = keys_at(kv_ref, lane, ys)
    v = with_ones(at, values_at(kv_ref, lane, ys), zk, ys, lane)
    key_pos = positions(at, zk, ys, lane, 256)
    for mate in range(MATES):
        weights = jnp.exp2(scores_of(queries_of(q_refs, mate), k))
        weights = keep(key_pos <= query_positions(at, mate), weights, 0.0)
        sum_ref[rows_of(mate), :] += mix(weights, v)


def fold_whole(q_refs, sum_ref, k, v):
    for mate in range(MATES):
        sum_ref[rows_of(mate), :] += mix(jnp.exp2(scores_of(queries_of(q_refs, mate), k)), v)


def fold_piece(at, q_refs, sum_ref, kv_ref, hops):
    zh, y, _, zl, c = at
    zk = (zh * 4 + zl + jnp.where(c == 0, 8 - hops, hops)) % 8

    @pl.when(zk // 4 < zh)
    def _():
        def lane_of(lane, carry):
            k = kv_ref[lane, :, :, :HEAD].reshape(512, HEAD)
            v = with_ones(at, kv_ref[lane, :, :, HEAD:].reshape(512, HEAD), zk, 0, lane)
            fold_whole(q_refs, sum_ref, k, v)
            return carry

        lax.fori_loop(0, 2, lane_of, 0)

    @pl.when(zk // 4 == zh)
    def _():
        def part(n, carry):
            fold_part(at, q_refs, sum_ref, kv_ref, zk, n // 2 * 4, n % 2)
            return carry

        lax.fori_loop(0, (y // 4 + 1) * 2, part, 0)


def half_kernel(at_ref, kv_ref, out_ref):
    out_ref[...] = kv_ref[:, pl.ds(at_ref[4] * 4, 4)]


def open_kernel(at_ref, *refs):
    q_refs, (own_ref, sum_ref) = refs[:4], refs[4:]
    at = zh, y, x, zl, c = tuple(at_ref[i] for i in range(5))
    sum_ref[...] = jnp.zeros(sum_ref.shape, f32)

    @pl.when(c * 4 <= y)
    def _():
        def part(lane, carry):
            fold_part(at, q_refs, sum_ref, own_ref, zh * 4 + zl, c * 4, lane)
            return carry

        lax.fori_loop(0, 2, part, 0)


def next_kernel(hops, at_ref, *refs):
    q_refs, (kv_ref, before_ref, sum_ref) = refs[:4], refs[4:]
    at = tuple(at_ref[i] for i in range(5))
    if hops not in (1, 2, 3):
        sum_ref[...] = before_ref[...]
    fold_piece(at, q_refs, sum_ref, kv_ref, hops)


def close_kernel(at_ref, *refs):
    q_refs, pieces, (far_ref, sum_ref, out_ref, kv_ref, q_copy) = refs[:4], refs[4:8], refs[8:]
    at = zh, y, x, zl, c = tuple(at_ref[i] for i in range(5))
    z = zh * 4 + zl
    far = (z + 4) % 8
    half = c * 4

    @pl.when(far // 4 < zh)
    def _():
        k = far_ref[:, :, :, :HEAD].reshape(512, HEAD)
        v = [with_ones(at, far_ref[lane, :, :, HEAD:].reshape(256, HEAD), far, half, lane) for lane in range(2)]
        fold_whole(q_refs, sum_ref, k, jnp.concatenate(v, axis=0))

    number_row = lax.broadcasted_iota(jnp.int32, (1, HEAD), 1)
    where_z = [(z + jnp.where(c == 0, 8 - n, n)) % 8 for n in range(5)]
    first_y = [half, 0, 0, 0, half]
    lowest = SEQ
    for zk, ys in zip(where_z, first_y):
        lowest = jnp.minimum(lowest, ((zk // 4 * 8 + ys) * 32 + x * 8 + zk % 4 * 2) * TOK)
    lowest = jnp.maximum(lowest, SINKS)

    def finish(mate, peak):
        number = number_of(at, mate)
        out_ref[number, :ROWS, :] = sum_ref[rows_of(mate), :HEAD].astype(bf16)
        total = sum_ref[rows_of(mate), HEAD:]
        high = total.astype(bf16).astype(f32)
        stat = jnp.where(number_row == 0, peak, jnp.where(number_row == 1, high, total - high))
        stat = jnp.concatenate([stat, jnp.zeros((TOK, HEAD), f32)], axis=0)
        tiles = [stat[chunk * 128 : (chunk + 1) * 128].T[:4] for chunk in range(CHUNKS)]
        out_ref[number, STAT : STAT + 16, :] = jnp.concatenate(tiles, axis=0).astype(bf16)

    lost = jnp.zeros((TOK, HEAD), jnp.bool_)
    for mate in range(MATES):
        total = sum_ref[rows_of(mate), HEAD:].reshape(GROUP, TOK, HEAD)
        seen = query_positions(at, mate) >= lowest
        top = jnp.max(total, axis=0)
        low = jnp.min(total, axis=0)
        lost = lost | jnp.logical_not(top < 2.0**120) | jnp.logical_not((low > 2.0**-40) | jnp.logical_not(seen))
        finish(mate, 0.0)

    @pl.when(jnp.max(jnp.where(lost, 1.0, 0.0)) > 0.0)
    def _():
        for n in range(4):
            kv_ref[n] = pieces[n][...]
            q_copy[2 * n * ROWS : 2 * (n + 1) * ROWS, :] = q_refs[n][...]
        kv_ref[4, :, :4] = far_ref[...]
        kv_ref[4, :, 4:] = far_ref[...]

        def again(mate, carry):
            rows = rows_of(mate)
            sum_ref[rows, :] = jnp.zeros((ROWS, 2 * HEAD), f32)

            def step(tile, peak):
                n, lane, ys = tile // 4, tile // 2 % 2, tile % 2 * 4
                zk = (z + jnp.where(c == 0, 8 - n, n)) % 8
                k = keys_at(kv_ref.at[n], lane, ys)
                v = with_ones(at, values_at(kv_ref.at[n], lane, ys), zk, ys, lane)
                key_pos = positions(at, zk, ys, lane, 256)
                mine = jnp.where((n == 0) | (n == 4), jnp.where(ys == half, 0, SEQ), 0)
                visible = (key_pos + mine <= query_positions(at, mate)) & (key_pos >= SINKS)
                scores = keep(visible, scores_of(q_copy[rows, :], k), masked)
                fresh = jnp.maximum(peak, jnp.max(scores, axis=1, keepdims=True))
                weights = keep(visible, jnp.exp2(scores - fresh), 0.0)
                sum_ref[rows, :] = sum_ref[rows, :] * jnp.exp2(peak - fresh) + mix(weights, v)
                return fresh

            peak = lax.fori_loop(0, 20, step, jnp.full((ROWS, 1), masked, f32))
            sent = peak.astype(bf16).astype(f32)
            sum_ref[rows, :] = sum_ref[rows, :] * jnp.exp2(peak - sent)
            finish(mate, sent)
            return carry

        lax.fori_loop(0, MATES, again, 0)

    both = far_ref[0, 0, :8, :].astype(f32)
    for n in range(4):
        both = jnp.where(where_z[n] == 0, pieces[n][0, 0, :8, :].astype(f32), both)
    both = both[:SINKS]
    both = jnp.concatenate([both[:, :HEAD], both[:, HEAD:], jnp.zeros((8, HEAD), f32)], axis=0).astype(bf16)
    for mate in range(MATES):
        out_ref[mate, EXTRA:, :] = both


def combine_kernel(at, q_ref, got_ref, out_ref):
    zh, y, x, zl, c = (at[i] for i in range(5))
    first = ((zh * 8 + y) * 32 + x * 8 + zl * 2 + c) * TOK
    extra = got_ref[jnp.where(zh * 4 + zl <= 4, 0, 1), EXTRA:, :]
    values = extra.astype(f32)
    number = lax.broadcasted_iota(jnp.int32, (8, 128), 0)
    token = lax.broadcasted_iota(jnp.int32, (8, 128), 1) & (TOK - 1)
    visible = (number < SINKS) & (number <= first + token)
    for chunk in range(CHUNKS):
        size = min(128, ROWS - 128 * chunk)
        rows = slice(128 * chunk, 128 * chunk + size)
        q = q_ref[rows, :]
        if size < 128:
            q = jnp.concatenate([q, q], axis=0)
        scores = lax.dot_general(extra, q, (((1,), (1,)), ((), ())), preferred_element_type=f32)[:8] * SCALE
        scores = jnp.where(visible, scores, masked)
        stats = [got_ref[k, STAT : STAT + 16, :].astype(f32)[4 * chunk : 4 * chunk + 4] for k in range(MATES)]
        peaks = jnp.concatenate([s[0:1] for s in stats], axis=0)
        totals = jnp.concatenate([s[1:2] + s[2:3] for s in stats], axis=0)
        peak = jnp.maximum(jnp.max(scores, axis=0, keepdims=True), jnp.max(peaks, axis=0, keepdims=True))
        sinks = jnp.where(visible, jnp.exp2(scores - peak), 0.0)
        shares = jnp.exp2(peaks - peak)
        total = jnp.sum(sinks, axis=0, keepdims=True) + jnp.sum(shares * totals, axis=0, keepdims=True)
        table = jnp.concatenate([shares / total, sinks / total, jnp.zeros((112, 128), f32)], axis=0)
        factors = table.T[:size]
        mixed = jnp.zeros((size, HEAD), f32)
        for k in range(MATES):
            mixed = mixed + factors[:, k : k + 1] * got_ref[k, rows, :].astype(f32)
        for s in range(SINKS):
            mixed = mixed + factors[:, MATES + s : MATES + s + 1] * values[SINKS + s : SINKS + s + 1, :]
        out_ref[rows, :] = mixed.astype(bf16)


def onward(piece):
    pairs = [(2 * z, (2 * z + 2) % 16) for z in range(8)] + [(2 * z + 1, (2 * z + 15) % 16) for z in range(8)]
    return lax.ppermute(piece, (*Z, "c"), pairs)


def along_x(block, hops):
    return lax.ppermute(block, "x", [(n, (n + hops) % 4) for n in range(4)])


def cost(keys):
    count = ALL_ROWS * keys
    return pl.CostEstimate(flops=count * 4 * HEAD * 2, transcendentals=count, bytes_accessed=1 << 20)


def per_device(queries, keys, values):
    at = jnp.stack(place()).astype(jnp.int32)
    q = queries.reshape(ROWS, HEAD)
    q_own = lax.all_gather(q, "c", axis=0, tiled=True)
    kv = jnp.broadcast_to(jnp.concatenate([keys, values], axis=1)[None], (8, TOK, 2 * HEAD))
    own = lax.all_to_all(kv, "y", 0, 0, tiled=True)
    q_all = [q_own]
    for hops in (1, -1, 2):
        q_all.append(along_x(q_own, hops))
    own = lax.all_gather(own, "c", axis=0)
    smem = pl.BlockSpec(memory_space=pltpu.SMEM)
    vmem = pl.BlockSpec(memory_space=pltpu.VMEM)
    piece1 = onward(own)
    piece2 = onward(piece1)
    piece3 = onward(piece2)
    part = pl.pallas_call(
        half_kernel,
        out_shape=pltpu.VMEM((2, 4, TOK, 2 * HEAD), bf16),
        in_specs=[smem, vmem],
        out_specs=vmem,
        compiler_params=pltpu.CompilerParams(vmem_limit_bytes=4 << 20),
        name="half",
    )(at, piece3)
    far = onward(part)
    roomy = pltpu.CompilerParams(vmem_limit_bytes=32 << 20)
    sums = pltpu.VMEM((ALL_ROWS, 2 * HEAD), f32)
    total = pl.pallas_call(
        open_kernel,
        out_shape=sums,
        in_specs=[smem] + [vmem] * 5,
        out_specs=vmem,
        cost_estimate=cost(512),
        compiler_params=roomy,
        name="open",
    )(at, *q_all, own)
    for hops, piece in ((1, piece1), (2, piece2), (3, piece3)):
        total = pl.pallas_call(
            functools.partial(next_kernel, hops),
            out_shape=sums,
            in_specs=[smem] + [vmem] * 6,
            out_specs=vmem,
            input_output_aliases={6: 0} if hops in (1, 2, 3) else {},
            cost_estimate=cost(1024),
            compiler_params=roomy,
        )(at, *q_all, piece, total)
    partial = pl.pallas_call(
        close_kernel,
        out_shape=jax.ShapeDtypeStruct((MATES, PAYLOAD, HEAD), bf16),
        in_specs=[smem] + [vmem] * 10,
        out_specs=vmem,
        scratch_shapes=[pltpu.VMEM((5, 2, 8, TOK, 2 * HEAD), bf16), pltpu.VMEM((ALL_ROWS, HEAD), bf16)],
        cost_estimate=cost(512),
        compiler_params=roomy,
        name="close",
    )(at, *q_all, own, piece1, piece2, piece3, far, total)
    got = lax.all_to_all(partial, TEAM, 0, 0, tiled=True)
    out = pl.pallas_call(
        combine_kernel,
        out_shape=jax.ShapeDtypeStruct((ROWS, HEAD), bf16),
        in_specs=[smem, vmem, vmem],
        out_specs=vmem,
        compiler_params=roomy,
        name="combine",
    )(at, q, got)
    return out.reshape(GROUP, TOK, HEAD)


def solution(mesh):
    split = Mesh(mesh.devices.reshape(SIZES), AXES)
    shard = P(None, AXES, None)
    return jax.shard_map(
        per_device,
        mesh=split,
        in_specs=(shard, P(AXES, None), P(AXES, None)),
        out_specs=shard,
        check_vma=False,
    )
```

profile of v0, /device:TPU:1, one launch (start us, length us, event | category | flops | bytes accessed | tf_op | source)
XLA Modules:
  0.0 112.6 jit_solution(2754602726983285055)
XLA Ops:
  0.0 0.7 pad_maximum_fusion
  0.8 17.0 %all_to_all.10 = bf16[8,64,256]{2,1,0:T(8,128)(2,1)S(1)} all-to-all(bf16[8,64,256]{2,1,0:T(8,128)(2,1)S(1)} %broadcast_in_dim.2), channel_id=1, replica_groups=mesh['zh'=2,'y'=8,'x'=4,'zl'=4,'c'=2] {'y'}, dimensions={0} | all-to-all | bytes 524288 | tf_op jit(solution)/shard_map/all_to_all | solution.py:297
  17.7 5.1 %all-gather = bf16[16,64,256]{2,1,0:T(8,128)(2,1)S(1)} all-gather(bf16[8,64,256]{2,1,0:T(8,128)(2,1)S(1)} %all_to_all.10), channel_id=2, replica_groups=mesh['zh'=2,'y'=8,'x'=4,'zl'=4,'c'=2] {'c'}, dimensions={0}, use_global_device_ids=true | all-gather | bytes 786432 | tf_op jit(solution)/shard_map/all_gather | solution.py:301
  22.8 10.7 %collective-permute-start.3 = (bf16[2,8,64,256]{3,2,1,0:T(8,128)(2,1)S(1)}, bf16[2,8,64,256]{3,2,1,0:T(8,128)(2,1)S(1)}, u32[]{:S(2)}, u32[]{:S(2)}) collective-permute-start(bf16[2,8,64,256]{3,2,1,0:T(8,128)(2,1)S(1)} %bitcast.8), channel_id=1, source_target_pairs={{0,2},{2,4},{4,6},{6,256},{256,258},{258,260},{260,262},{262,0},{1... | collective-permute-start | bytes 1572872 | tf_op jit(solution)/shard_map/ppermute | solution.py:280
  33.5 6.1 %collective-permute-done.3.refs_4_.refs_5_ = bf16[2,8,64,256]{3,2,1,0:T(8,128)(2,1)S(1)} collective-permute-done((bf16[2,8,64,256]{3,2,1,0:T(8,128)(2,1)S(1)}, bf16[2,8,64,256]{3,2,1,0:T(8,128)(2,1)S(1)}, u32[]{:S(2)}, u32[]{:S(2)}) %collective-permute-start.3) | collective-permute-done | bytes 524320 | tf_op jit(solution)/shard_map/ppermute | solution.py:280
  39.6 5.0 %collective-permute-start.4 = (bf16[2,8,64,256]{3,2,1,0:T(8,128)(2,1)S(1)}, bf16[2,8,64,256]{3,2,1,0:T(8,128)(2,1)S(1)}, u32[]{:S(2)}, u32[]{:S(2)}) collective-permute-start(bf16[2,8,64,256]{3,2,1,0:T(8,128)(2,1)S(1)} %collective-permute-done.3.refs_4_.refs_5_), channel_id=1, source_target_pairs={{0,2},{2,4},{4,6},{6,256},{256,258},{258,260},{260,262},{262,0},{1... | collective-permute-start | bytes 1572872 | tf_op jit(solution)/shard_map/ppermute | solution.py:280
  44.6 2.2 %all_gather.9.refs_0_ = bf16[896,128]{1,0:T(8,128)(2,1)S(1)} all-gather(bf16[448,128]{1,0:T(8,128)(2,1)} %bitcast.11), channel_id=1, replica_groups=mesh['zh'=2,'y'=8,'x'=4,'zl'=4,'c'=2] {'c'}, dimensions={0}, use_global_device_ids=true | all-gather | bytes 344064 | tf_op jit(solution)/shard_map/all_gather | solution.py:295
  46.8 3.1 %collective-permute-start = (bf16[896,128]{1,0:T(8,128)(2,1)S(1)}, bf16[896,128]{1,0:T(8,128)(2,1)S(1)}, u32[]{:S(2)}, u32[]{:S(2)}) collective-permute-start(bf16[896,128]{1,0:T(8,128)(2,1)S(1)} %all_gather.9.refs_0_), channel_id=1, source_target_pairs={{0,8},{8,16},{16,24},{24,0},{1,9},{9,17},{17,25},{25,1},{2,10},{10... | collective-permute-start | bytes 688136 | tf_op jit(solution)/shard_map/ppermute | solution.py:284
  49.9 3.4 %collective-permute-start.1 = (bf16[896,128]{1,0:T(8,128)(2,1)S(1)}, bf16[896,128]{1,0:T(8,128)(2,1)S(1)}, u32[]{:S(2)}, u32[]{:S(2)}) collective-permute-start(bf16[896,128]{1,0:T(8,128)(2,1)S(1)} %all_gather.9.refs_0_), channel_id=1, source_target_pairs={{0,24},{8,0},{16,8},{24,16},{1,25},{9,1},{17,9},{25,17},{2,26},{10... | collective-permute-start | bytes 688136 | tf_op jit(solution)/shard_map/ppermute | solution.py:284
  53.3 3.4 %collective-permute-start.2 = (bf16[896,128]{1,0:T(8,128)(2,1)S(1)}, bf16[896,128]{1,0:T(8,128)(2,1)S(1)}, u32[]{:S(2)}, u32[]{:S(2)}) collective-permute-start(bf16[896,128]{1,0:T(8,128)(2,1)S(1)} %all_gather.9.refs_0_), channel_id=1, source_target_pairs={{0,16},{8,24},{16,0},{24,8},{1,17},{9,25},{17,1},{25,9},{2,18},{10... | collective-permute-start | bytes 688136 | tf_op jit(solution)/shard_map/ppermute | solution.py:284
  56.8 0.1 stack.23.at_ref.at
  56.8 0.1 collective-permute-done.refs_1_
  56.9 1.6 %collective-permute-done.1.refs_2_ = bf16[896,128]{1,0:T(8,128)(2,1)S(1)} collective-permute-done((bf16[896,128]{1,0:T(8,128)(2,1)S(1)}, bf16[896,128]{1,0:T(8,128)(2,1)S(1)}, u32[]{:S(2)}, u32[]{:S(2)}) %collective-permute-start.1) | collective-permute-done | bytes 229408 | tf_op jit(solution)/shard_map/ppermute | solution.py:284
  58.5 4.6 %collective-permute-done.2.refs_3_ = bf16[896,128]{1,0:T(8,128)(2,1)S(1)} collective-permute-done((bf16[896,128]{1,0:T(8,128)(2,1)S(1)}, bf16[896,128]{1,0:T(8,128)(2,1)S(1)}, u32[]{:S(2)}, u32[]{:S(2)}) %collective-permute-start.2) | collective-permute-done | bytes 229408 | tf_op jit(solution)/shard_map/ppermute | solution.py:284
  63.2 0.8 open.1.refs_5_
  63.9 0.0 collective-permute-done.4.refs_4_.refs_6_
  63.9 2.9 %collective-permute-start.5 = (bf16[2,8,64,256]{3,2,1,0:T(8,128)(2,1)S(1)}, bf16[2,8,64,256]{3,2,1,0:T(8,128)(2,1)S(1)}, u32[]{:S(2)}, u32[]{:S(2)}) collective-permute-start(bf16[2,8,64,256]{3,2,1,0:T(8,128)(2,1)S(1)} %collective-permute-done.4.refs_4_.refs_6_), channel_id=1, source_target_pairs={{0,2},{2,4},{4,6},{6,256},{256,258},{258,260},{260,262},{262,0},{1... | collective-permute-start | bytes 1572872 | tf_op jit(solution)/shard_map/ppermute | solution.py:280
  66.8 3.1 %shard_map.37.refs_5_ = f32[3584,256]{1,0:T(8,128)S(1)} custom-call(s32[5]{0:T(128)S(1)} %stack.23.at_ref.at, bf16[896,128]{1,0:T(8,128)(2,1)S(1)} %all_gather.9.refs_0_, bf16[896,128]{1,0:T(8,128)(2,1)S(1)} %collective-permute-done.refs_1_, bf16[896,128]{1,0:T(8,128)(2,1)S(1)} %collective-permute-done.1.refs_2_, ...), custom_call_target="tpu_custom_call", output_to_operand_aliasing={{}: (6, {})} | custom-call | flops 3758096384 | bytes 1048576 | tf_op jit(solution)/shard_map/pallas_call | solution.py:328
  69.9 3.1 %shard_map.38.refs_5_ = f32[3584,256]{1,0:T(8,128)S(1)} custom-call(s32[5]{0:T(128)S(1)} %stack.23.at_ref.at, bf16[896,128]{1,0:T(8,128)(2,1)S(1)} %all_gather.9.refs_0_, bf16[896,128]{1,0:T(8,128)(2,1)S(1)} %collective-permute-done.refs_1_, bf16[896,128]{1,0:T(8,128)(2,1)S(1)} %collective-permute-done.1.refs_2_, ...), custom_call_target="tpu_custom_call", output_to_operand_aliasing={{}: (6, {})} | custom-call | flops 3758096384 | bytes 1048576 | tf_op jit(solution)/shard_map/pallas_call | solution.py:328
  73.0 0.9 collective-permute-done.5.kv_ref.refs_4_.refs_7_
  73.9 0.6 half.1
  74.4 5.3 %collective-permute-start.6 = (bf16[2,4,64,256]{3,2,1,0:T(8,128)(2,1)S(1)}, bf16[2,4,64,256]{3,2,1,0:T(8,128)(2,1)S(1)}, u32[]{:S(2)}, u32[]{:S(2)}) collective-permute-start(bf16[2,4,64,256]{3,2,1,0:T(8,128)(2,1)S(1)} %half.1), channel_id=1, source_target_pairs={{0,2},{2,4},{4,6},{6,256},{256,258},{258,260},{260,262},{262,0},{1... | collective-permute-start | bytes 786440 | tf_op jit(solution)/shard_map/ppermute | solution.py:280
  79.8 3.2 %shard_map.39.refs_9_ = f32[3584,256]{1,0:T(8,128)S(1)} custom-call(s32[5]{0:T(128)S(1)} %stack.23.at_ref.at, bf16[896,128]{1,0:T(8,128)(2,1)S(1)} %all_gather.9.refs_0_, bf16[896,128]{1,0:T(8,128)(2,1)S(1)} %collective-permute-done.refs_1_, bf16[896,128]{1,0:T(8,128)(2,1)S(1)} %collective-permute-done.1.refs_2_, ...), custom_call_target="tpu_custom_call", output_to_operand_aliasing={{}: (6, {})} | custom-call | flops 3758096384 | bytes 1048576 | tf_op jit(solution)/shard_map/pallas_call | solution.py:328
  83.0 0.0 copy-start
  83.0 0.0 collective-permute-done.6.refs_8_
  83.1 1.5 %close.1 = bf16[8,480,128]{2,1,0:T(8,128)(2,1)S(1)} custom-call(s32[5]{0:T(128)S(1)} %stack.23.at_ref.at, bf16[896,128]{1,0:T(8,128)(2,1)S(1)} %all_gather.9.refs_0_, bf16[896,128]{1,0:T(8,128)(2,1)S(1)} %collective-permute-done.refs_1_, bf16[896,128]{1,0:T(8,128)(2,1)S(1)} %collective-permute-done.1.refs_2_, ...), custom_call_target="tpu_custom_call" | custom-call | flops 1879048192 | bytes 1048576 | tf_op jit(solution)/shard_map/close/pallas_call | solution.py:337
  84.5 25.6 %all_to_all.11.got_ref = bf16[8,480,128]{2,1,0:T(8,128)(2,1)S(1)} all-to-all(bf16[8,480,128]{2,1,0:T(8,128)(2,1)S(1)} %close.1), channel_id=1, replica_groups=mesh['zh'=2,'y'=8,'x'=4,'zl'=4,'c'=2] {'x','c'}, dimensions={0} | all-to-all | bytes 1966080 | tf_op jit(solution)/shard_map/all_to_all | solution.py:347
  110.2 0.0 copy-done
  110.2 2.5 %combine.1 = bf16[448,128]{1,0:T(8,128)(2,1)} custom-call(s32[5]{0:T(128)S(1)} %stack.23.at_ref.at, bf16[448,128]{1,0:T(8,128)(2,1)S(1)} %bitcast.12, bf16[8,480,128]{2,1,0:T(8,128)(2,1)S(1)} %all_to_all.11.got_ref), custom_call_target="tpu_custom_call" | custom-call | tf_op jit(solution)/shard_map/combine/pallas_call | solution.py:348
  (1 shorter events, 0.0 us)
Async XLA Ops:
  22.8 16.8 %collective-permute-start.3 = (bf16[2,8,64,256]{3,2,1,0:T(8,128)(2,1)S(1)}, bf16[2,8,64,256]{3,2,1,0:T(8,128)(2,1)S(1)}, u32[]{:S(2)}, u32[]{:S(2)}) collective-permute-start(bf16[2,8,64,256]{3,2,1,0:T(8,128)(2,1)S(1)} %bitcast.8), channel_id=1, source_target_pairs={{0,2},{2,4},{4,6},{6,256},{256,258},{258,260},{260,262},{262,0},{1... | collective-permute-start | bytes 1572872 | tf_op jit(solution)/shard_map/ppermute | solution.py:280
  39.6 24.3 %collective-permute-start.4 = (bf16[2,8,64,256]{3,2,1,0:T(8,128)(2,1)S(1)}, bf16[2,8,64,256]{3,2,1,0:T(8,128)(2,1)S(1)}, u32[]{:S(2)}, u32[]{:S(2)}) collective-permute-start(bf16[2,8,64,256]{3,2,1,0:T(8,128)(2,1)S(1)} %collective-permute-done.3.refs_4_.refs_5_), channel_id=1, source_target_pairs={{0,2},{2,4},{4,6},{6,256},{256,258},{258,260},{260,262},{262,0},{1... | collective-permute-start | bytes 1572872 | tf_op jit(solution)/shard_map/ppermute | solution.py:280
  46.8 10.1 %collective-permute-start = (bf16[896,128]{1,0:T(8,128)(2,1)S(1)}, bf16[896,128]{1,0:T(8,128)(2,1)S(1)}, u32[]{:S(2)}, u32[]{:S(2)}) collective-permute-start(bf16[896,128]{1,0:T(8,128)(2,1)S(1)} %all_gather.9.refs_0_), channel_id=1, source_target_pairs={{0,8},{8,16},{16,24},{24,0},{1,9},{9,17},{17,25},{25,1},{2,10},{10... | collective-permute-start | bytes 688136 | tf_op jit(solution)/shard_map/ppermute | solution.py:284
  49.9 8.6 %collective-permute-start.1 = (bf16[896,128]{1,0:T(8,128)(2,1)S(1)}, bf16[896,128]{1,0:T(8,128)(2,1)S(1)}, u32[]{:S(2)}, u32[]{:S(2)}) collective-permute-start(bf16[896,128]{1,0:T(8,128)(2,1)S(1)} %all_gather.9.refs_0_), channel_id=1, source_target_pairs={{0,24},{8,0},{16,8},{24,16},{1,25},{9,1},{17,9},{25,17},{2,26},{10... | collective-permute-start | bytes 688136 | tf_op jit(solution)/shard_map/ppermute | solution.py:284
  53.3 9.9 %collective-permute-start.2 = (bf16[896,128]{1,0:T(8,128)(2,1)S(1)}, bf16[896,128]{1,0:T(8,128)(2,1)S(1)}, u32[]{:S(2)}, u32[]{:S(2)}) collective-permute-start(bf16[896,128]{1,0:T(8,128)(2,1)S(1)} %all_gather.9.refs_0_), channel_id=1, source_target_pairs={{0,16},{8,24},{16,0},{24,8},{1,17},{9,25},{17,1},{25,9},{2,18},{10... | collective-permute-start | bytes 688136 | tf_op jit(solution)/shard_map/ppermute | solution.py:284
  63.9 9.9 %collective-permute-start.5 = (bf16[2,8,64,256]{3,2,1,0:T(8,128)(2,1)S(1)}, bf16[2,8,64,256]{3,2,1,0:T(8,128)(2,1)S(1)}, u32[]{:S(2)}, u32[]{:S(2)}) collective-permute-start(bf16[2,8,64,256]{3,2,1,0:T(8,128)(2,1)S(1)} %collective-permute-done.4.refs_4_.refs_6_), channel_id=1, source_target_pairs={{0,2},{2,4},{4,6},{6,256},{256,258},{258,260},{260,262},{262,0},{1... | collective-permute-start | bytes 1572872 | tf_op jit(solution)/shard_map/ppermute | solution.py:280
  74.4 8.6 %collective-permute-start.6 = (bf16[2,4,64,256]{3,2,1,0:T(8,128)(2,1)S(1)}, bf16[2,4,64,256]{3,2,1,0:T(8,128)(2,1)S(1)}, u32[]{:S(2)}, u32[]{:S(2)}) collective-permute-start(bf16[2,4,64,256]{3,2,1,0:T(8,128)(2,1)S(1)} %half.1), channel_id=1, source_target_pairs={{0,2},{2,4},{4,6},{6,256},{256,258},{258,260},{260,262},{262,0},{1... | collective-permute-start | bytes 786440 | tf_op jit(solution)/shard_map/ppermute | solution.py:280
  83.0 27.1 %copy-start = (bf16[7,64,128]{2,1,0:T(8,128)(2,1)S(1)}, bf16[7,64,128]{2,1,0:T(8,128)(2,1)}, u32[]{:S(2)}) copy-start(bf16[7,64,128]{2,1,0:T(8,128)(2,1)} %param.3) | copy-start | bytes 344068
where the time goes:
time: 113 us
  blocking collectives  49.9 us (44%)
  starting transfers between devices  33.8 us (30%)
  Pallas kernels  14.6 us (13%)
  waiting for transfers between devices  13.4 us (12%)
    all_to_all x1, blocking collectives, per_device(): got = lax.all_to_all(partial, TEAM, 0, 0, tiled=True)  25.6 us
    ppermute x4, starting transfers between devices, onward(): return lax.ppermute(piece, (*Z, 'c'), pairs)  23.9 us
    all_to_all x1, blocking collectives, per_device(): own = lax.all_to_all(kv, 'y', 0, 0, tiled=True)  17 us
    ppermute x3, starting transfers between devices, along_x(): return lax.ppermute(block, 'x', [(n, (n + hops) % 4) for n in range(4)])  9.92 us
    pallas_call x3, Pallas kernels, per_device(): pl.pallas_call(functools.partial(next_kernel, hops), out_shape=sums, in_s...  9.36 us
    ppermute x4, waiting for transfers between devices, onward(): return lax.ppermute(piece, (*Z, 'c'), pairs)  7.06 us
    ppermute x3, waiting for transfers between devices, along_x(): return lax.ppermute(block, 'x', [(n, (n + hops) % 4) for n in range(4)])  6.31 us
    all_gather x1, blocking collectives, per_device(): own = lax.all_gather(own, 'c', axis=0)  5.09 us
  transfers between devices with their start and end apart: 7, of which 5 were waited for; matrix products, arithmetic and copies ran while one was open for 0% of the time, Pallas kernels for 9%

commit v1 on v0

--- a/solution.py
+++ b/solution.py
@@ -133,51 +133,45 @@
         lax.fori_loop(0, (y // 4 + 1) * 2, part, 0)
 
 
-def half_kernel(at_ref, kv_ref, out_ref):
-    out_ref[...] = kv_ref[:, pl.ds(at_ref[4] * 4, 4)]
-
-
 def open_kernel(at_ref, *refs):
-    q_refs, (own_ref, sum_ref) = refs[:4], refs[4:]
+    q_refs, (own_ref, sum_ref, kv_ref) = refs[:4], refs[4:]
     at = zh, y, x, zl, c = tuple(at_ref[i] for i in range(5))
+    kv_ref[c] = own_ref[...]
     sum_ref[...] = jnp.zeros(sum_ref.shape, f32)
 
-    @pl.when(c * 4 <= y)
-    def _():
-        def part(lane, carry):
-            fold_part(at, q_refs, sum_ref, own_ref, zh * 4 + zl, c * 4, lane)
-            return carry
-
-        lax.fori_loop(0, 2, part, 0)
+    def part(n, carry):
+        fold_part(at, q_refs, sum_ref, kv_ref, zh * 4 + zl, n * 4, c)
+        return carry
+
+    lax.fori_loop(0, y // 4 + 1, part, 0)
 
 
 def next_kernel(hops, at_ref, *refs):
-    q_refs, (kv_ref, before_ref, sum_ref) = refs[:4], refs[4:]
+    q_refs, (mine_ref, other_ref, before_ref, sum_ref, kv_ref) = refs[:4], refs[4:]
     at = tuple(at_ref[i] for i in range(5))
-    if hops not in (1, 2, 3):
-        sum_ref[...] = before_ref[...]
+    kv_ref[at[4]] = mine_ref[...]
+    kv_ref[1 - at[4]] = other_ref[...]
     fold_piece(at, q_refs, sum_ref, kv_ref, hops)
 
 
 def close_kernel(at_ref, *refs):
-    q_refs, pieces, (far_ref, sum_ref, out_ref, kv_ref, q_copy) = refs[:4], refs[4:8], refs[8:]
+    q_refs, mines, others, (sum_ref, out_ref, kv_ref, q_copy) = refs[:4], refs[4:9], refs[9:12], refs[12:]
+    far_ref = mines[4]
     at = zh, y, x, zl, c = tuple(at_ref[i] for i in range(5))
     z = zh * 4 + zl
     far = (z + 4) % 8
-    half = c * 4
 
     @pl.when(far // 4 < zh)
     def _():
-        k = far_ref[:, :, :, :HEAD].reshape(512, HEAD)
-        v = [with_ones(at, far_ref[lane, :, :, HEAD:].reshape(256, HEAD), far, half, lane) for lane in range(2)]
-        fold_whole(q_refs, sum_ref, k, jnp.concatenate(v, axis=0))
+        k = far_ref[:, :, :HEAD].reshape(512, HEAD)
+        v = with_ones(at, far_ref[:, :, HEAD:].reshape(512, HEAD), far, 0, c)
+        fold_whole(q_refs, sum_ref, k, v)
 
     number_row = lax.broadcasted_iota(jnp.int32, (1, HEAD), 1)
     where_z = [(z + jnp.where(c == 0, 8 - n, n)) % 8 for n in range(5)]
-    first_y = [half, 0, 0, 0, half]
     lowest = SEQ
-    for zk, ys in zip(where_z, first_y):
-        lowest = jnp.minimum(lowest, ((zk // 4 * 8 + ys) * 32 + x * 8 + zk % 4 * 2) * TOK)
+    for zk, lane in zip(where_z, (c, 0, 0, 0, c)):
+        lowest = jnp.minimum(lowest, (zk // 4 * 256 + x * 8 + zk % 4 * 2 + lane) * TOK)
     lowest = jnp.maximum(lowest, SINKS)
 
     def finish(mate, peak):
@@ -201,11 +195,11 @@
 
     @pl.when(jnp.max(jnp.where(lost, 1.0, 0.0)) > 0.0)
     def _():
+        for n in range(5):
+            kv_ref[n, c] = mines[n][...]
+            kv_ref[n, 1 - c] = others[n - 1][...] if 0 < n < 4 else mines[n][...]
         for n in range(4):
-            kv_ref[n] = pieces[n][...]
             q_copy[2 * n * ROWS : 2 * (n + 1) * ROWS, :] = q_refs[n][...]
-        kv_ref[4, :, :4] = far_ref[...]
-        kv_ref[4, :, 4:] = far_ref[...]
 
         def again(mate, carry):
             rows = rows_of(mate)
@@ -217,7 +211,7 @@
                 k = keys_at(kv_ref.at[n], lane, ys)
                 v = with_ones(at, values_at(kv_ref.at[n], lane, ys), zk, ys, lane)
                 key_pos = positions(at, zk, ys, lane, 256)
-                mine = jnp.where((n == 0) | (n == 4), jnp.where(ys == half, 0, SEQ), 0)
+                mine = jnp.where((n == 0) | (n == 4), jnp.where(lane == c, 0, SEQ), 0)
                 visible = (key_pos + mine <= query_positions(at, mate)) & (key_pos >= SINKS)
                 scores = keep(visible, scores_of(q_copy[rows, :], k), masked)
                 fresh = jnp.maximum(peak, jnp.max(scores, axis=1, keepdims=True))
@@ -233,9 +227,12 @@
 
         lax.fori_loop(0, MATES, again, 0)
 
-    both = far_ref[0, 0, :8, :].astype(f32)
+    both = far_ref[0, :8, :].astype(f32)
     for n in range(4):
-        both = jnp.where(where_z[n] == 0, pieces[n][0, 0, :8, :].astype(f32), both)
+        first = mines[n][0, :8, :].astype(f32)
+        if n > 0:
+            first = jnp.where(c == 0, first, others[n - 1][0, :8, :].astype(f32))
+        both = jnp.where(where_z[n] == 0, first, both)
     both = both[:SINKS]
     both = jnp.concatenate([both[:, :HEAD], both[:, HEAD:], jnp.zeros((8, HEAD), f32)], axis=0).astype(bf16)
     for mate in range(MATES):
@@ -298,21 +295,14 @@
     q_all = [q_own]
     for hops in (1, -1, 2):
         q_all.append(along_x(q_own, hops))
-    own = lax.all_gather(own, "c", axis=0)
     smem = pl.BlockSpec(memory_space=pltpu.SMEM)
     vmem = pl.BlockSpec(memory_space=pltpu.VMEM)
-    piece1 = onward(own)
-    piece2 = onward(piece1)
-    piece3 = onward(piece2)
-    part = pl.pallas_call(
-        half_kernel,
-        out_shape=pltpu.VMEM((2, 4, TOK, 2 * HEAD), bf16),
-        in_specs=[smem, vmem],
-        out_specs=vmem,
-        compiler_params=pltpu.CompilerParams(vmem_limit_bytes=4 << 20),
-        name="half",
-    )(at, piece3)
-    far = onward(part)
+    mines = [own]
+    for _ in range(1, 5):
+        mines.append(onward(mines[-1]))
+    others = [lax.ppermute(own, "c", [(0, 1), (1, 0)])]
+    for _ in range(1, 4):
+        others.append(onward(others[-1]))
     roomy = pltpu.CompilerParams(vmem_limit_bytes=32 << 20)
     sums = pltpu.VMEM((ALL_ROWS, 2 * HEAD), f32)
     total = pl.pallas_call(
@@ -320,30 +310,32 @@
         out_shape=sums,
         in_specs=[smem] + [vmem] * 5,
         out_specs=vmem,
+        scratch_shapes=[pltpu.VMEM((2, 8, TOK, 2 * HEAD), bf16)],
         cost_estimate=cost(512),
         compiler_params=roomy,
         name="open",
     )(at, *q_all, own)
-    for hops, piece in ((1, piece1), (2, piece2), (3, piece3)):
+    for hops in (1, 2, 3):
         total = pl.pallas_call(
             functools.partial(next_kernel, hops),
             out_shape=sums,
-            in_specs=[smem] + [vmem] * 6,
+            in_specs=[smem] + [vmem] * 7,
             out_specs=vmem,
-            input_output_aliases={6: 0} if hops in (1, 2, 3) else {},
+            input_output_aliases={7: 0},
+            scratch_shapes=[pltpu.VMEM((2, 8, TOK, 2 * HEAD), bf16)],
             cost_estimate=cost(1024),
             compiler_params=roomy,
-        )(at, *q_all, piece, total)
+        )(at, *q_all, mines[hops], others[hops], total)
     partial = pl.pallas_call(
         close_kernel,
         out_shape=jax.ShapeDtypeStruct((MATES, PAYLOAD, HEAD), bf16),
-        in_specs=[smem] + [vmem] * 10,
+        in_specs=[smem] + [vmem] * 13,
         out_specs=vmem,
         scratch_shapes=[pltpu.VMEM((5, 2, 8, TOK, 2 * HEAD), bf16), pltpu.VMEM((ALL_ROWS, HEAD), bf16)],
         cost_estimate=cost(512),
         compiler_params=roomy,
         name="close",
-    )(at, *q_all, own, piece1, piece2, piece3, far, total)
+    )(at, *q_all, *mines, *others[1:], total)
     got = lax.all_to_all(partial, TEAM, 0, 0, tiled=True)
     out = pl.pallas_call(
         combine_kernel,

time: 113 us -> 100 us (0.88)
  waiting for transfers between devices: 13.4 us -> 1.08 us
  blocking collectives: 49.9 us -> 40.3 us
  starting transfers between devices: 33.8 us -> 42 us
    ppermute x4 -> x7, waiting for transfers between devices: 7.06 us -> 0.02 us  [onward(): return lax.ppermute(piece, (*Z, 'c'), pairs)]
    ppermute x3, waiting for transfers between devices: 6.31 us -> 1.06 us  [along_x(): return lax.ppermute(block, 'x', [(n, (n + hops) % 4) for n in range(4)])]
    ppermute x0 -> x1, starting transfers between devices: none -> 5.19 us  [per_device(): others = [lax.ppermute(own, 'c', [(0, 1), (1, 0)])]]
    all_gather x1 -> x0, blocking collectives: 5.09 us -> none  [per_device(): own = lax.all_gather(own, 'c', axis=0)]
    all_to_all x1, blocking collectives: 25.6 us -> 21.1 us  [per_device(): got = lax.all_to_all(partial, TEAM, 0, 0, tiled=True)]
    ppermute x4 -> x7, starting transfers between devices: 23.9 us -> 26.9 us  [onward(): return lax.ppermute(piece, (*Z, 'c'), pairs)]
    pallas_call x1, Pallas kernels: 0.78 us -> 2.03 us  [per_device(): pl.pallas_call(open_kernel, out_shape=sums, in_specs=[smem] + [vmem] * 5,...]
  transfers between devices with their start and end apart: 7 -> 11, of which waited for: 5 -> 1; matrix products, arithmetic and copies ran while one was open for 0% -> 0% of each run, Pallas kernels for 9% -> 11%
where the time goes in v1:
time: 100 us; the launch traced here: 99.8 us
  starting transfers between devices  42 us (42%)
  blocking collectives  40.3 us (40%)
  Pallas kernels  15.4 us (15%)
  waiting for transfers between devices  1.08 us (1%)
    ppermute x7, starting transfers between devices, onward(): return lax.ppermute(piece, (*Z, 'c'), pairs)  26.9 us
    all_to_all x1, blocking collectives, per_device(): got = lax.all_to_all(partial, TEAM, 0, 0, tiled=True)  21.1 us
    all_to_all x1, blocking collectives, per_device(): own = lax.all_to_all(kv, 'y', 0, 0, tiled=True)  17 us
    ppermute x3, starting transfers between devices, along_x(): return lax.ppermute(block, 'x', [(n, (n + hops) % 4) for n in range(4)])  9.92 us
    pallas_call x3, Pallas kernels, per_device(): pl.pallas_call(functools.partial(next_kernel, hops), out_shape=sums, in_s...  9.42 us
    ppermute x1, starting transfers between devices, per_device(): others = [lax.ppermute(own, 'c', [(0, 1), (1, 0)])]  5.19 us
    pallas_call x1, Pallas kernels, per_device(): pl.pallas_call(combine_kernel, out_shape=jax.ShapeDtypeStruct((ROWS, HEAD...  2.47 us
    all_gather x1, blocking collectives, per_device(): q_own = lax.all_gather(q, 'c', axis=0, tiled=True)  2.18 us
  transfers between devices with their start and end apart: 11, of which 1 were waited for; matrix products, arithmetic and copies ran while one was open for 0% of the time, Pallas kernels for 11%

profile of v1, /device:TPU:1, one launch (start us, length us, event | category | flops | bytes accessed | tf_op | source)
XLA Modules:
  0.0 99.8 jit_solution(3670557707752893303)
XLA Ops:
  0.0 0.7 pad_maximum_fusion
  0.8 17.0 %all_to_all.10.refs_4_ = bf16[8,64,256]{2,1,0:T(8,128)(2,1)S(1)} all-to-all(bf16[8,64,256]{2,1,0:T(8,128)(2,1)S(1)} %broadcast_in_dim.2), channel_id=1, replica_groups=mesh['zh'=2,'y'=8,'x'=4,'zl'=4,'c'=2] {'y'}, dimensions={0} | all-to-all | bytes 524288 | tf_op jit(solution)/shard_map/all_to_all | solution.py:294
  17.7 5.2 %collective-permute-start.7 = (bf16[8,64,256]{2,1,0:T(8,128)(2,1)S(1)}, bf16[8,64,256]{2,1,0:T(8,128)(2,1)S(1)}, u32[]{:S(2)}, u32[]{:S(2)}) collective-permute-start(bf16[8,64,256]{2,1,0:T(8,128)(2,1)S(1)} %all_to_all.10.refs_4_), channel_id=1, source_target_pairs={{0,1},{1,0},{2,3},{3,2},{4,5},{5,4},{6,7},{7,6},{8,9},{9,8},{10,11... | collective-permute-start | bytes 786440 | tf_op jit(solution)/shard_map/ppermute | solution.py:303
  22.9 10.7 %collective-permute-start.3 = (bf16[8,64,256]{2,1,0:T(8,128)(2,1)S(1)}, bf16[8,64,256]{2,1,0:T(8,128)(2,1)S(1)}, u32[]{:S(2)}, u32[]{:S(2)}) collective-permute-start(bf16[8,64,256]{2,1,0:T(8,128)(2,1)S(1)} %all_to_all.10.refs_4_), channel_id=1, source_target_pairs={{0,2},{2,4},{4,6},{6,256},{256,258},{258,260},{260,262},{262,0},{1... | collective-permute-start | bytes 786440 | tf_op jit(solution)/shard_map/ppermute | solution.py:277
  33.6 2.2 %all_gather.3.refs_0_ = bf16[896,128]{1,0:T(8,128)(2,1)S(1)} all-gather(bf16[448,128]{1,0:T(8,128)(2,1)} %bitcast.7), channel_id=1, replica_groups=mesh['zh'=2,'y'=8,'x'=4,'zl'=4,'c'=2] {'c'}, dimensions={0}, use_global_device_ids=true | all-gather | bytes 344064 | tf_op jit(solution)/shard_map/all_gather | solution.py:292
  35.8 3.1 %collective-permute-start = (bf16[896,128]{1,0:T(8,128)(2,1)S(1)}, bf16[896,128]{1,0:T(8,128)(2,1)S(1)}, u32[]{:S(2)}, u32[]{:S(2)}) collective-permute-start(bf16[896,128]{1,0:T(8,128)(2,1)S(1)} %all_gather.3.refs_0_), channel_id=1, source_target_pairs={{0,8},{8,16},{16,24},{24,0},{1,9},{9,17},{17,25},{25,1},{2,10},{10... | collective-permute-start | bytes 688136 | tf_op jit(solution)/shard_map/ppermute | solution.py:281
  38.9 3.4 %collective-permute-start.1 = (bf16[896,128]{1,0:T(8,128)(2,1)S(1)}, bf16[896,128]{1,0:T(8,128)(2,1)S(1)}, u32[]{:S(2)}, u32[]{:S(2)}) collective-permute-start(bf16[896,128]{1,0:T(8,128)(2,1)S(1)} %all_gather.3.refs_0_), channel_id=1, source_target_pairs={{0,24},{8,0},{16,8},{24,16},{1,25},{9,1},{17,9},{25,17},{2,26},{10... | collective-permute-start | bytes 688136 | tf_op jit(solution)/shard_map/ppermute | solution.py:281
  42.3 3.4 %collective-permute-start.2 = (bf16[896,128]{1,0:T(8,128)(2,1)S(1)}, bf16[896,128]{1,0:T(8,128)(2,1)S(1)}, u32[]{:S(2)}, u32[]{:S(2)}) collective-permute-start(bf16[896,128]{1,0:T(8,128)(2,1)S(1)} %all_gather.3.refs_0_), channel_id=1, source_target_pairs={{0,16},{8,24},{16,0},{24,8},{1,17},{9,25},{17,1},{25,9},{2,18},{10... | collective-permute-start | bytes 688136 | tf_op jit(solution)/shard_map/ppermute | solution.py:281
  45.7 0.0 collective-permute-done.7
  45.8 2.2 %collective-permute-start.8 = (bf16[8,64,256]{2,1,0:T(8,128)(2,1)S(1)}, bf16[8,64,256]{2,1,0:T(8,128)(2,1)S(1)}, u32[]{:S(2)}, u32[]{:S(2)}) collective-permute-start(bf16[8,64,256]{2,1,0:T(8,128)(2,1)S(1)} %collective-permute-done.7), channel_id=1, source_target_pairs={{0,2},{2,4},{4,6},{6,256},{256,258},{258,260},{260,262},{262,0},{1... | collective-permute-start | bytes 786440 | tf_op jit(solution)/shard_map/ppermute | solution.py:277
  47.9 0.0 collective-permute-done.3.refs_4_.refs_5_
  48.0 3.0 %collective-permute-start.4 = (bf16[8,64,256]{2,1,0:T(8,128)(2,1)S(1)}, bf16[8,64,256]{2,1,0:T(8,128)(2,1)S(1)}, u32[]{:S(2)}, u32[]{:S(2)}) collective-permute-start(bf16[8,64,256]{2,1,0:T(8,128)(2,1)S(1)} %collective-permute-done.3.refs_4_.refs_5_), channel_id=1, source_target_pairs={{0,2},{2,4},{4,6},{6,256},{256,258},{258,260},{260,262},{262,0},{1... | collective-permute-start | bytes 786440 | tf_op jit(solution)/shard_map/ppermute | solution.py:277
  51.0 0.1 stack.23.at_ref.at
  51.1 0.0 collective-permute-done.refs_1_
  51.1 0.0 collective-permute-done.1.refs_2_
  51.1 1.1 %collective-permute-done.2.refs_3_ = bf16[896,128]{1,0:T(8,128)(2,1)S(1)} collective-permute-done((bf16[896,128]{1,0:T(8,128)(2,1)S(1)}, bf16[896,128]{1,0:T(8,128)(2,1)S(1)}, u32[]{:S(2)}, u32[]{:S(2)}) %collective-permute-start.2) | collective-permute-done | bytes 229408 | tf_op jit(solution)/shard_map/ppermute | solution.py:281
  52.1 2.0 %open.1.refs_6_ = f32[3584,256]{1,0:T(8,128)S(1)} custom-call(s32[5]{0:T(128)S(1)} %stack.23.at_ref.at, bf16[896,128]{1,0:T(8,128)(2,1)S(1)} %all_gather.3.refs_0_, bf16[896,128]{1,0:T(8,128)(2,1)S(1)} %collective-permute-done.refs_1_, bf16[896,128]{1,0:T(8,128)(2,1)S(1)} %collective-permute-done.1.refs_2_, ...), custom_call_target="tpu_custom_call" | custom-call | flops 1879048192 | bytes 1048576 | tf_op jit(solution)/shard_map/open/pallas_call | solution.py:308
  54.2 0.0 collective-permute-done.8.refs_5_.refs_9_
  54.2 2.2 %collective-permute-start.9 = (bf16[8,64,256]{2,1,0:T(8,128)(2,1)S(1)}, bf16[8,64,256]{2,1,0:T(8,128)(2,1)S(1)}, u32[]{:S(2)}, u32[]{:S(2)}) collective-permute-start(bf16[8,64,256]{2,1,0:T(8,128)(2,1)S(1)} %collective-permute-done.8.refs_5_.refs_9_), channel_id=1, source_target_pairs={{0,2},{2,4},{4,6},{6,256},{256,258},{258,260},{260,262},{262,0},{1... | collective-permute-start | bytes 786440 | tf_op jit(solution)/shard_map/ppermute | solution.py:277
  56.4 0.0 collective-permute-done.4.refs_4_.refs_6_
  56.4 2.9 %collective-permute-start.5 = (bf16[8,64,256]{2,1,0:T(8,128)(2,1)S(1)}, bf16[8,64,256]{2,1,0:T(8,128)(2,1)S(1)}, u32[]{:S(2)}, u32[]{:S(2)}) collective-permute-start(bf16[8,64,256]{2,1,0:T(8,128)(2,1)S(1)} %collective-permute-done.4.refs_4_.refs_6_), channel_id=1, source_target_pairs={{0,2},{2,4},{4,6},{6,256},{256,258},{258,260},{260,262},{262,0},{1... | collective-permute-start | bytes 786440 | tf_op jit(solution)/shard_map/ppermute | solution.py:277
  59.3 3.1 %shard_map.37.refs_6_ = f32[3584,256]{1,0:T(8,128)S(1)} custom-call(s32[5]{0:T(128)S(1)} %stack.23.at_ref.at, bf16[896,128]{1,0:T(8,128)(2,1)S(1)} %all_gather.3.refs_0_, bf16[896,128]{1,0:T(8,128)(2,1)S(1)} %collective-permute-done.refs_1_, bf16[896,128]{1,0:T(8,128)(2,1)S(1)} %collective-permute-done.1.refs_2_, ...), custom_call_target="tpu_custom_call", output_to_operand_aliasing={{}: (7, {})} | custom-call | flops 3758096384 | bytes 1048576 | tf_op jit(solution)/shard_map/pallas_call | solution.py:319
  62.4 0.0 collective-permute-done.9.refs_5_.refs_10_
  62.4 4.0 %collective-permute-start.10 = (bf16[8,64,256]{2,1,0:T(8,128)(2,1)S(1)}, bf16[8,64,256]{2,1,0:T(8,128)(2,1)S(1)}, u32[]{:S(2)}, u32[]{:S(2)}) collective-permute-start(bf16[8,64,256]{2,1,0:T(8,128)(2,1)S(1)} %collective-permute-done.9.refs_5_.refs_10_), channel_id=1, source_target_pairs={{0,2},{2,4},{4,6},{6,256},{256,258},{258,260},{260,262},{262,0},{1... | collective-permute-start | bytes 786440 | tf_op jit(solution)/shard_map/ppermute | solution.py:277
  66.4 0.0 collective-permute-done.5.refs_4_.refs_7_
  66.4 1.9 %collective-permute-start.6 = (bf16[8,64,256]{2,1,0:T(8,128)(2,1)S(1)}, bf16[8,64,256]{2,1,0:T(8,128)(2,1)S(1)}, u32[]{:S(2)}, u32[]{:S(2)}) collective-permute-start(bf16[8,64,256]{2,1,0:T(8,128)(2,1)S(1)} %collective-permute-done.5.refs_4_.refs_7_), channel_id=1, source_target_pairs={{0,2},{2,4},{4,6},{6,256},{256,258},{258,260},{260,262},{262,0},{1... | collective-permute-start | bytes 786440 | tf_op jit(solution)/shard_map/ppermute | solution.py:277
  68.4 3.1 %shard_map.38.refs_6_ = f32[3584,256]{1,0:T(8,128)S(1)} custom-call(s32[5]{0:T(128)S(1)} %stack.23.at_ref.at, bf16[896,128]{1,0:T(8,128)(2,1)S(1)} %all_gather.3.refs_0_, bf16[896,128]{1,0:T(8,128)(2,1)S(1)} %collective-permute-done.refs_1_, bf16[896,128]{1,0:T(8,128)(2,1)S(1)} %collective-permute-done.1.refs_2_, ...), custom_call_target="tpu_custom_call", output_to_operand_aliasing={{}: (7, {})} | custom-call | flops 3758096384 | bytes 1048576 | tf_op jit(solution)/shard_map/pallas_call | solution.py:319
  71.5 3.3 %shard_map.39.refs_12_ = f32[3584,256]{1,0:T(8,128)S(1)} custom-call(s32[5]{0:T(128)S(1)} %stack.23.at_ref.at, bf16[896,128]{1,0:T(8,128)(2,1)S(1)} %all_gather.3.refs_0_, bf16[896,128]{1,0:T(8,128)(2,1)S(1)} %collective-permute-done.refs_1_, bf16[896,128]{1,0:T(8,128)(2,1)S(1)} %collective-permute-done.1.refs_2_, ...), custom_call_target="tpu_custom_call", output_to_operand_aliasing={{}: (7, {})} | custom-call | flops 3758096384 | bytes 1048576 | tf_op jit(solution)/shard_map/pallas_call | solution.py:319
  74.7 0.0 copy-start
  74.7 1.5 %close.1 = bf16[8,480,128]{2,1,0:T(8,128)(2,1)S(1)} custom-call(s32[5]{0:T(128)S(1)} %stack.23.at_ref.at, bf16[896,128]{1,0:T(8,128)(2,1)S(1)} %all_gather.3.refs_0_, bf16[896,128]{1,0:T(8,128)(2,1)S(1)} %collective-permute-done.refs_1_, bf16[896,128]{1,0:T(8,128)(2,1)S(1)} %collective-permute-done.1.refs_2_, ...), custom_call_target="tpu_custom_call" | custom-call | flops 1879048192 | bytes 1048576 | tf_op jit(solution)/shard_map/close/pallas_call | solution.py:329
  76.2 21.1 %all_to_all.11.got_ref = bf16[8,480,128]{2,1,0:T(8,128)(2,1)S(1)} all-to-all(bf16[8,480,128]{2,1,0:T(8,128)(2,1)S(1)} %close.1), channel_id=1, replica_groups=mesh['zh'=2,'y'=8,'x'=4,'zl'=4,'c'=2] {'x','c'}, dimensions={0} | all-to-all | bytes 1966080 | tf_op jit(solution)/shard_map/all_to_all | solution.py:339
  97.4 2.5 %combine.1 = bf16[448,128]{1,0:T(8,128)(2,1)} custom-call(s32[5]{0:T(128)S(1)} %stack.23.at_ref.at, bf16[448,128]{1,0:T(8,128)(2,1)S(1)} %bitcast.8, bf16[8,480,128]{2,1,0:T(8,128)(2,1)S(1)} %all_to_all.11.got_ref), custom_call_target="tpu_custom_call" | custom-call | tf_op jit(solution)/shard_map/combine/pallas_call | solution.py:340
  (4 shorter events, 0.0 us)
Async XLA Ops:
  17.7 28.0 %collective-permute-start.7 = (bf16[8,64,256]{2,1,0:T(8,128)(2,1)S(1)}, bf16[8,64,256]{2,1,0:T(8,128)(2,1)S(1)}, u32[]{:S(2)}, u32[]{:S(2)}) collective-permute-start(bf16[8,64,256]{2,1,0:T(8,128)(2,1)S(1)} %all_to_all.10.refs_4_), channel_id=1, source_target_pairs={{0,1},{1,0},{2,3},{3,2},{4,5},{5,4},{6,7},{7,6},{8,9},{9,8},{10,11... | collective-permute-start | bytes 786440 | tf_op jit(solution)/shard_map/ppermute | solution.py:303
  22.9 25.0 %collective-permute-start.3 = (bf16[8,64,256]{2,1,0:T(8,128)(2,1)S(1)}, bf16[8,64,256]{2,1,0:T(8,128)(2,1)S(1)}, u32[]{:S(2)}, u32[]{:S(2)}) collective-permute-start(bf16[8,64,256]{2,1,0:T(8,128)(2,1)S(1)} %all_to_all.10.refs_4_), channel_id=1, source_target_pairs={{0,2},{2,4},{4,6},{6,256},{256,258},{258,260},{260,262},{262,0},{1... | collective-permute-start | bytes 786440 | tf_op jit(solution)/shard_map/ppermute | solution.py:277
  35.8 15.3 %collective-permute-start = (bf16[896,128]{1,0:T(8,128)(2,1)S(1)}, bf16[896,128]{1,0:T(8,128)(2,1)S(1)}, u32[]{:S(2)}, u32[]{:S(2)}) collective-permute-start(bf16[896,128]{1,0:T(8,128)(2,1)S(1)} %all_gather.3.refs_0_), channel_id=1, source_target_pairs={{0,8},{8,16},{16,24},{24,0},{1,9},{9,17},{17,25},{25,1},{2,10},{10... | collective-permute-start | bytes 688136 | tf_op jit(solution)/shard_map/ppermute | solution.py:281
  38.9 12.2 %collective-permute-start.1 = (bf16[896,128]{1,0:T(8,128)(2,1)S(1)}, bf16[896,128]{1,0:T(8,128)(2,1)S(1)}, u32[]{:S(2)}, u32[]{:S(2)}) collective-permute-start(bf16[896,128]{1,0:T(8,128)(2,1)S(1)} %all_gather.3.refs_0_), channel_id=1, source_target_pairs={{0,24},{8,0},{16,8},{24,16},{1,25},{9,1},{17,9},{25,17},{2,26},{10... | collective-permute-start | bytes 688136 | tf_op jit(solution)/shard_map/ppermute | solution.py:281
  42.3 9.9 %collective-permute-start.2 = (bf16[896,128]{1,0:T(8,128)(2,1)S(1)}, bf16[896,128]{1,0:T(8,128)(2,1)S(1)}, u32[]{:S(2)}, u32[]{:S(2)}) collective-permute-start(bf16[896,128]{1,0:T(8,128)(2,1)S(1)} %all_gather.3.refs_0_), channel_id=1, source_target_pairs={{0,16},{8,24},{16,0},{24,8},{1,17},{9,25},{17,1},{25,9},{2,18},{10... | collective-permute-start | bytes 688136 | tf_op jit(solution)/shard_map/ppermute | solution.py:281
  45.8 8.4 %collective-permute-start.8 = (bf16[8,64,256]{2,1,0:T(8,128)(2,1)S(1)}, bf16[8,64,256]{2,1,0:T(8,128)(2,1)S(1)}, u32[]{:S(2)}, u32[]{:S(2)}) collective-permute-start(bf16[8,64,256]{2,1,0:T(8,128)(2,1)S(1)} %collective-permute-done.7), channel_id=1, source_target_pairs={{0,2},{2,4},{4,6},{6,256},{256,258},{258,260},{260,262},{262,0},{1... | collective-permute-start | bytes 786440 | tf_op jit(solution)/shard_map/ppermute | solution.py:277
  48.0 8.4 %collective-permute-start.4 = (bf16[8,64,256]{2,1,0:T(8,128)(2,1)S(1)}, bf16[8,64,256]{2,1,0:T(8,128)(2,1)S(1)}, u32[]{:S(2)}, u32[]{:S(2)}) collective-permute-start(bf16[8,64,256]{2,1,0:T(8,128)(2,1)S(1)} %collective-permute-done.3.refs_4_.refs_5_), channel_id=1, source_target_pairs={{0,2},{2,4},{4,6},{6,256},{256,258},{258,260},{260,262},{262,0},{1... | collective-permute-start | bytes 786440 | tf_op jit(solution)/shard_map/ppermute | solution.py:277
  54.2 8.2 %collective-permute-start.9 = (bf16[8,64,256]{2,1,0:T(8,128)(2,1)S(1)}, bf16[8,64,256]{2,1,0:T(8,128)(2,1)S(1)}, u32[]{:S(2)}, u32[]{:S(2)}) collective-permute-start(bf16[8,64,256]{2,1,0:T(8,128)(2,1)S(1)} %collective-permute-done.8.refs_5_.refs_9_), channel_id=1, source_target_pairs={{0,2},{2,4},{4,6},{6,256},{256,258},{258,260},{260,262},{262,0},{1... | collective-permute-start | bytes 786440 | tf_op jit(solution)/shard_map/ppermute | solution.py:277
  56.4 10.0 %collective-permute-start.5 = (bf16[8,64,256]{2,1,0:T(8,128)(2,1)S(1)}, bf16[8,64,256]{2,1,0:T(8,128)(2,1)S(1)}, u32[]{:S(2)}, u32[]{:S(2)}) collective-permute-start(bf16[8,64,256]{2,1,0:T(8,128)(2,1)S(1)} %collective-permute-done.4.refs_4_.refs_6_), channel_id=1, source_target_pairs={{0,2},{2,4},{4,6},{6,256},{256,258},{258,260},{260,262},{262,0},{1... | collective-permute-start | bytes 786440 | tf_op jit(solution)/shard_map/ppermute | solution.py:277
  62.4 9.0 %collective-permute-start.10 = (bf16[8,64,256]{2,1,0:T(8,128)(2,1)S(1)}, bf16[8,64,256]{2,1,0:T(8,128)(2,1)S(1)}, u32[]{:S(2)}, u32[]{:S(2)}) collective-permute-start(bf16[8,64,256]{2,1,0:T(8,128)(2,1)S(1)} %collective-permute-done.9.refs_5_.refs_10_), channel_id=1, source_target_pairs={{0,2},{2,4},{4,6},{6,256},{256,258},{258,260},{260,262},{262,0},{1... | collective-permute-start | bytes 786440 | tf_op jit(solution)/shard_map/ppermute | solution.py:277
  66.4 8.3 %collective-permute-start.6 = (bf16[8,64,256]{2,1,0:T(8,128)(2,1)S(1)}, bf16[8,64,256]{2,1,0:T(8,128)(2,1)S(1)}, u32[]{:S(2)}, u32[]{:S(2)}) collective-permute-start(bf16[8,64,256]{2,1,0:T(8,128)(2,1)S(1)} %collective-permute-done.5.refs_4_.refs_7_), channel_id=1, source_target_pairs={{0,2},{2,4},{4,6},{6,256},{256,258},{258,260},{260,262},{262,0},{1... | collective-permute-start | bytes 786440 | tf_op jit(solution)/shard_map/ppermute | solution.py:277
  74.7 22.6 %copy-start = (bf16[7,64,128]{2,1,0:T(8,128)(2,1)S(1)}, bf16[7,64,128]{2,1,0:T(8,128)(2,1)}, u32[]{:S(2)}) copy-start(bf16[7,64,128]{2,1,0:T(8,128)(2,1)} %param.3) | copy-start | bytes 344068

commit v2 on v1

--- a/solution.py
+++ b/solution.py
@@ -95,63 +95,25 @@
     return ref[lane, pl.ds(ys, 4), :, HEAD:].reshape(256, HEAD)
 
 
-def fold_part(at, q_refs, sum_ref, kv_ref, zk, ys, lane):
-    k = keys_at(kv_ref, lane, ys)
-    v = with_ones(at, values_at(kv_ref, lane, ys), zk, ys, lane)
-    key_pos = positions(at, zk, ys, lane, 256)
-    for mate in range(MATES):
-        weights = jnp.exp2(scores_of(queries_of(q_refs, mate), k))
-        weights = keep(key_pos <= query_positions(at, mate), weights, 0.0)
-        sum_ref[rows_of(mate), :] += mix(weights, v)
-
-
-def fold_whole(q_refs, sum_ref, k, v):
-    for mate in range(MATES):
-        sum_ref[rows_of(mate), :] += mix(jnp.exp2(scores_of(queries_of(q_refs, mate), k)), v)
-
-
-def fold_piece(at, q_refs, sum_ref, kv_ref, hops):
-    zh, y, _, zl, c = at
+def fold_piece(at, q_refs, sum_ref, kv_ref, zk, lane):
+    @pl.when(zk // 4 <= at[0])
+    def _():
+        k = kv_ref[:, :, :HEAD].reshape(512, HEAD)
+        v = with_ones(at, kv_ref[:, :, HEAD:].reshape(512, HEAD), zk, 0, lane)
+        key_pos = positions(at, zk, 0, lane, 512)
+        for mate in range(MATES):
+            weights = jnp.exp2(scores_of(queries_of(q_refs, mate), k))
+            weights = keep(key_pos <= query_positions(at, mate), weights, 0.0)
+            sum_ref[rows_of(mate), :] += mix(weights, v)
+
+
+def step_kernel(hops, other, at_ref, *refs):
+    q_refs, kv_ref, sum_ref = refs[:4], refs[4], refs[-1]
+    at = zh, y, x, zl, c = tuple(at_ref[i] for i in range(5))
+    if hops == 0:
+        sum_ref[...] = jnp.zeros(sum_ref.shape, f32)
     zk = (zh * 4 + zl + jnp.where(c == 0, 8 - hops, hops)) % 8
-
-    @pl.when(zk // 4 < zh)
-    def _():
-        def lane_of(lane, carry):
-            k = kv_ref[lane, :, :, :HEAD].reshape(512, HEAD)
-            v = with_ones(at, kv_ref[lane, :, :, HEAD:].reshape(512, HEAD), zk, 0, lane)
-            fold_whole(q_refs, sum_ref, k, v)
-            return carry
-
-        lax.fori_loop(0, 2, lane_of, 0)
-
-    @pl.when(zk // 4 == zh)
-    def _():
-        def part(n, carry):
-            fold_part(at, q_refs, sum_ref, kv_ref, zk, n // 2 * 4, n % 2)
-            return carry
-
-        lax.fori_loop(0, (y // 4 + 1) * 2, part, 0)
-
-
-def open_kernel(at_ref, *refs):
-    q_refs, (own_ref, sum_ref, kv_ref) = refs[:4], refs[4:]
-    at = zh, y, x, zl, c = tuple(at_ref[i] for i in range(5))
-    kv_ref[c] = own_ref[...]
-    sum_ref[...] = jnp.zeros(sum_ref.shape, f32)
-
-    def part(n, carry):
-        fold_part(at, q_refs, sum_ref, kv_ref, zh * 4 + zl, n * 4, c)
-        return carry
-
-    lax.fori_loop(0, y // 4 + 1, part, 0)
-
-
-def next_kernel(hops, at_ref, *refs):
-    q_refs, (mine_ref, other_ref, before_ref, sum_ref, kv_ref) = refs[:4], refs[4:]
-    at = tuple(at_ref[i] for i in range(5))
-    kv_ref[at[4]] = mine_ref[...]
-    kv_ref[1 - at[4]] = other_ref[...]
-    fold_piece(at, q_refs, sum_ref, kv_ref, hops)
+    fold_piece(at, q_refs, sum_ref, kv_ref, zk, 1 - c if other else c)
 
 
 def close_kernel(at_ref, *refs):
@@ -161,11 +123,7 @@
     z = zh * 4 + zl
     far = (z + 4) % 8
 
-    @pl.when(far // 4 < zh)
-    def _():
-        k = far_ref[:, :, :HEAD].reshape(512, HEAD)
-        v = with_ones(at, far_ref[:, :, HEAD:].reshape(512, HEAD), far, 0, c)
-        fold_whole(q_refs, sum_ref, k, v)
+    fold_piece(at, q_refs, sum_ref, far_ref, far, c)
 
     number_row = lax.broadcasted_iota(jnp.int32, (1, HEAD), 1)
     where_z = [(z + jnp.where(c == 0, 8 - n, n)) % 8 for n in range(5)]
@@ -305,27 +263,19 @@
         others.append(onward(others[-1]))
     roomy = pltpu.CompilerParams(vmem_limit_bytes=32 << 20)
     sums = pltpu.VMEM((ALL_ROWS, 2 * HEAD), f32)
-    total = pl.pallas_call(
-        open_kernel,
-        out_shape=sums,
-        in_specs=[smem] + [vmem] * 5,
-        out_specs=vmem,
-        scratch_shapes=[pltpu.VMEM((2, 8, TOK, 2 * HEAD), bf16)],
-        cost_estimate=cost(512),
-        compiler_params=roomy,
-        name="open",
-    )(at, *q_all, own)
-    for hops in (1, 2, 3):
-        total = pl.pallas_call(
-            functools.partial(next_kernel, hops),
-            out_shape=sums,
-            in_specs=[smem] + [vmem] * 7,
-            out_specs=vmem,
-            input_output_aliases={7: 0},
-            scratch_shapes=[pltpu.VMEM((2, 8, TOK, 2 * HEAD), bf16)],
-            cost_estimate=cost(1024),
-            compiler_params=roomy,
-        )(at, *q_all, mines[hops], others[hops], total)
+    total = ()
+    for hops, other in ((0, 0), (1, 0), (1, 1), (2, 0), (2, 1), (3, 0), (3, 1)):
+        total = (
+            pl.pallas_call(
+                functools.partial(step_kernel, hops, other),
+                out_shape=sums,
+                in_specs=[smem] + [vmem] * (5 + len(total)),
+                out_specs=vmem,
+                input_output_aliases={6: 0} if total else {},
+                cost_estimate=cost(512),
+                compiler_params=roomy,
+            )(at, *q_all, (others if other else mines)[hops], *total),
+        )
     partial = pl.pallas_call(
         close_kernel,
         out_shape=jax.ShapeDtypeStruct((MATES, PAYLOAD, HEAD), bf16),
@@ -335,7 +285,7 @@
         cost_estimate=cost(512),
         compiler_params=roomy,
         name="close",
-    )(at, *q_all, *mines, *others[1:], total)
+    )(at, *q_all, *mines, *others[1:], *total)
     got = lax.all_to_all(partial, TEAM, 0, 0, tiled=True)
     out = pl.pallas_call(
         combine_kernel,

time: 100 us -> 104 us (1.040)
  Pallas kernels: 15.4 us -> 23.5 us
  blocking collectives: 40.3 us -> 37.8 us
  starting transfers between devices: 42 us -> 40.5 us
  waiting for transfers between devices: 1.08 us -> 0.03 us
    pallas_call x4 -> x7, Pallas kernels: 11.5 us -> 19.6 us  [per_device(): pl.pallas_call(functools.partial(step_kernel, hops, other), out_shape=sum...]
    all_to_all x1, blocking collectives: 21.1 us -> 18.7 us  [per_device(): got = lax.all_to_all(partial, TEAM, 0, 0, tiled=True)]
    ppermute x7, starting transfers between devices: 26.9 us -> 25.4 us  [onward(): return lax.ppermute(piece, (*Z, 'c'), pairs)]
    ppermute x3, waiting for transfers between devices: 1.06 us -> 0.01 us  [along_x(): return lax.ppermute(block, 'x', [(n, (n + hops) % 4) for n in range(4)])]
  transfers between devices with their start and end apart: 11 -> 11, of which waited for: 1 -> 0; matrix products, arithmetic and copies ran while one was open for 0% -> 0% of each run, Pallas kernels for 11% -> 19%
where the time goes in v2:
time: 104 us; the launch traced here: 103 us
  starting transfers between devices  40.5 us (39%)
  blocking collectives  37.8 us (36%)
  Pallas kernels  23.5 us (23%)
    ppermute x7, starting transfers between devices, onward(): return lax.ppermute(piece, (*Z, 'c'), pairs)  25.4 us
    pallas_call x7, Pallas kernels, per_device(): pl.pallas_call(functools.partial(step_kernel, hops, other), out_shape=sum...  19.6 us
    all_to_all x1, blocking collectives, per_device(): got = lax.all_to_all(partial, TEAM, 0, 0, tiled=True)  18.7 us
    all_to_all x1, blocking collectives, per_device(): own = lax.all_to_all(kv, 'y', 0, 0, tiled=True)  17 us
    ppermute x3, starting transfers between devices, along_x(): return lax.ppermute(block, 'x', [(n, (n + hops) % 4) for n in range(4)])  9.92 us
    ppermute x1, starting transfers between devices, per_device(): others = [lax.ppermute(own, 'c', [(0, 1), (1, 0)])]  5.19 us
    pallas_call x1, Pallas kernels, per_device(): pl.pallas_call(combine_kernel, out_shape=jax.ShapeDtypeStruct((ROWS, HEAD...  2.47 us
    all_gather x1, blocking collectives, per_device(): q_own = lax.all_gather(q, 'c', axis=0, tiled=True)  2.18 us
  transfers between devices with their start and end apart: 11, of which 0 were waited for; matrix products, arithmetic and copies ran while one was open for 0% of the time, Pallas kernels for 19%

profile of v2, /device:TPU:1, one launch (start us, length us, event | category | flops | bytes accessed | tf_op | source)
XLA Modules:
  0.0 103.0 jit_solution(16629163089052890108)
XLA Ops:
  0.0 0.7 pad_maximum_fusion
  0.8 17.0 %all_to_all.10.refs_4_ = bf16[8,64,256]{2,1,0:T(8,128)(2,1)S(1)} all-to-all(bf16[8,64,256]{2,1,0:T(8,128)(2,1)S(1)} %broadcast_in_dim.2), channel_id=1, replica_groups=mesh['zh'=2,'y'=8,'x'=4,'zl'=4,'c'=2] {'y'}, dimensions={0} | all-to-all | bytes 524288 | tf_op jit(solution)/shard_map/all_to_all | solution.py:252
  17.7 5.2 %collective-permute-start.7 = (bf16[8,64,256]{2,1,0:T(8,128)(2,1)S(1)}, bf16[8,64,256]{2,1,0:T(8,128)(2,1)S(1)}, u32[]{:S(2)}, u32[]{:S(2)}) collective-permute-start(bf16[8,64,256]{2,1,0:T(8,128)(2,1)S(1)} %all_to_all.10.refs_4_), channel_id=1, source_target_pairs={{0,1},{1,0},{2,3},{3,2},{4,5},{5,4},{6,7},{7,6},{8,9},{9,8},{10,11... | collective-permute-start | bytes 786440 | tf_op jit(solution)/shard_map/ppermute | solution.py:261
  22.9 2.2 %all_gather.3.refs_0_ = bf16[896,128]{1,0:T(8,128)(2,1)S(1)} all-gather(bf16[448,128]{1,0:T(8,128)(2,1)} %bitcast.7), channel_id=1, replica_groups=mesh['zh'=2,'y'=8,'x'=4,'zl'=4,'c'=2] {'c'}, dimensions={0}, use_global_device_ids=true | all-gather | bytes 344064 | tf_op jit(solution)/shard_map/all_gather | solution.py:250
  25.1 3.1 %collective-permute-start = (bf16[896,128]{1,0:T(8,128)(2,1)S(1)}, bf16[896,128]{1,0:T(8,128)(2,1)S(1)}, u32[]{:S(2)}, u32[]{:S(2)}) collective-permute-start(bf16[896,128]{1,0:T(8,128)(2,1)S(1)} %all_gather.3.refs_0_), channel_id=1, source_target_pairs={{0,8},{8,16},{16,24},{24,0},{1,9},{9,17},{17,25},{25,1},{2,10},{10... | collective-permute-start | bytes 688136 | tf_op jit(solution)/shard_map/ppermute | solution.py:239
  28.2 3.4 %collective-permute-start.1 = (bf16[896,128]{1,0:T(8,128)(2,1)S(1)}, bf16[896,128]{1,0:T(8,128)(2,1)S(1)}, u32[]{:S(2)}, u32[]{:S(2)}) collective-permute-start(bf16[896,128]{1,0:T(8,128)(2,1)S(1)} %all_gather.3.refs_0_), channel_id=1, source_target_pairs={{0,24},{8,0},{16,8},{24,16},{1,25},{9,1},{17,9},{25,17},{2,26},{10... | collective-permute-start | bytes 688136 | tf_op jit(solution)/shard_map/ppermute | solution.py:239
  31.6 3.4 %collective-permute-start.2 = (bf16[896,128]{1,0:T(8,128)(2,1)S(1)}, bf16[896,128]{1,0:T(8,128)(2,1)S(1)}, u32[]{:S(2)}, u32[]{:S(2)}) collective-permute-start(bf16[896,128]{1,0:T(8,128)(2,1)S(1)} %all_gather.3.refs_0_), channel_id=1, source_target_pairs={{0,16},{8,24},{16,0},{24,8},{1,17},{9,25},{17,1},{25,9},{2,18},{10... | collective-permute-start | bytes 688136 | tf_op jit(solution)/shard_map/ppermute | solution.py:239
  35.1 10.7 %collective-permute-start.3 = (bf16[8,64,256]{2,1,0:T(8,128)(2,1)S(1)}, bf16[8,64,256]{2,1,0:T(8,128)(2,1)S(1)}, u32[]{:S(2)}, u32[]{:S(2)}) collective-permute-start(bf16[8,64,256]{2,1,0:T(8,128)(2,1)S(1)} %all_to_all.10.refs_4_), channel_id=1, source_target_pairs={{0,2},{2,4},{4,6},{6,256},{256,258},{258,260},{260,262},{262,0},{1... | collective-permute-start | bytes 786440 | tf_op jit(solution)/shard_map/ppermute | solution.py:235
  45.8 0.1 stack.23.at_ref.at
  45.8 2.2 %collective-permute-start.8 = (bf16[8,64,256]{2,1,0:T(8,128)(2,1)S(1)}, bf16[8,64,256]{2,1,0:T(8,128)(2,1)S(1)}, u32[]{:S(2)}, u32[]{:S(2)}) collective-permute-start(bf16[8,64,256]{2,1,0:T(8,128)(2,1)S(1)} %collective-permute-done.7), channel_id=1, source_target_pairs={{0,2},{2,4},{4,6},{6,256},{256,258},{258,260},{260,262},{262,0},{1... | collective-permute-start | bytes 786440 | tf_op jit(solution)/shard_map/ppermute | solution.py:235
  48.0 0.0 collective-permute-done.refs_1_
  48.0 0.0 collective-permute-done.1.refs_2_
  48.0 2.9 %shard_map.37.refs_5_ = f32[3584,256]{1,0:T(8,128)S(1)} custom-call(s32[5]{0:T(128)S(1)} %stack.23.at_ref.at, bf16[896,128]{1,0:T(8,128)(2,1)S(1)} %all_gather.3.refs_0_, bf16[896,128]{1,0:T(8,128)(2,1)S(1)} %collective-permute-done.refs_1_, bf16[896,128]{1,0:T(8,128)(2,1)S(1)} %collective-permute-done.1.refs_2_, ...), custom_call_target="tpu_custom_call" | custom-call | flops 1879048192 | bytes 1048576 | tf_op jit(solution)/shard_map/pallas_call | solution.py:269
  50.9 0.0 collective-permute-done.3.refs_4_.refs_5_
  50.9 4.1 %collective-permute-start.4 = (bf16[8,64,256]{2,1,0:T(8,128)(2,1)S(1)}, bf16[8,64,256]{2,1,0:T(8,128)(2,1)S(1)}, u32[]{:S(2)}, u32[]{:S(2)}) collective-permute-start(bf16[8,64,256]{2,1,0:T(8,128)(2,1)S(1)} %collective-permute-done.3.refs_4_.refs_5_), channel_id=1, source_target_pairs={{0,2},{2,4},{4,6},{6,256},{256,258},{258,260},{260,262},{262,0},{1... | collective-permute-start | bytes 786440 | tf_op jit(solution)/shard_map/ppermute | solution.py:235
  55.0 2.8 %shard_map.38.refs_5_ = f32[3584,256]{1,0:T(8,128)S(1)} custom-call(s32[5]{0:T(128)S(1)} %stack.23.at_ref.at, bf16[896,128]{1,0:T(8,128)(2,1)S(1)} %all_gather.3.refs_0_, bf16[896,128]{1,0:T(8,128)(2,1)S(1)} %collective-permute-done.refs_1_, bf16[896,128]{1,0:T(8,128)(2,1)S(1)} %collective-permute-done.1.refs_2_, ...), custom_call_target="tpu_custom_call", output_to_operand_aliasing={{}: (6, {})} | custom-call | flops 1879048192 | bytes 1048576 | tf_op jit(solution)/shard_map/pallas_call | solution.py:269
  57.8 2.2 %collective-permute-start.9 = (bf16[8,64,256]{2,1,0:T(8,128)(2,1)S(1)}, bf16[8,64,256]{2,1,0:T(8,128)(2,1)S(1)}, u32[]{:S(2)}, u32[]{:S(2)}) collective-permute-start(bf16[8,64,256]{2,1,0:T(8,128)(2,1)S(1)} %collective-permute-done.8.refs_4_.refs_9_), channel_id=1, source_target_pairs={{0,2},{2,4},{4,6},{6,256},{256,258},{258,260},{260,262},{262,0},{1... | collective-permute-start | bytes 786440 | tf_op jit(solution)/shard_map/ppermute | solution.py:235
  60.0 2.8 %shard_map.39.refs_5_ = f32[3584,256]{1,0:T(8,128)S(1)} custom-call(s32[5]{0:T(128)S(1)} %stack.23.at_ref.at, bf16[896,128]{1,0:T(8,128)(2,1)S(1)} %all_gather.3.refs_0_, bf16[896,128]{1,0:T(8,128)(2,1)S(1)} %collective-permute-done.refs_1_, bf16[896,128]{1,0:T(8,128)(2,1)S(1)} %collective-permute-done.1.refs_2_, ...), custom_call_target="tpu_custom_call", output_to_operand_aliasing={{}: (6, {})} | custom-call | flops 1879048192 | bytes 1048576 | tf_op jit(solution)/shard_map/pallas_call | solution.py:269
  62.7 0.0 collective-permute-done.4.refs_4_.refs_6_
  62.8 2.2 %collective-permute-start.5 = (bf16[8,64,256]{2,1,0:T(8,128)(2,1)S(1)}, bf16[8,64,256]{2,1,0:T(8,128)(2,1)S(1)}, u32[]{:S(2)}, u32[]{:S(2)}) collective-permute-start(bf16[8,64,256]{2,1,0:T(8,128)(2,1)S(1)} %collective-permute-done.4.refs_4_.refs_6_), channel_id=1, source_target_pairs={{0,2},{2,4},{4,6},{6,256},{256,258},{258,260},{260,262},{262,0},{1... | collective-permute-start | bytes 786440 | tf_op jit(solution)/shard_map/ppermute | solution.py:235
  64.9 2.8 %shard_map.40.refs_5_ = f32[3584,256]{1,0:T(8,128)S(1)} custom-call(s32[5]{0:T(128)S(1)} %stack.23.at_ref.at, bf16[896,128]{1,0:T(8,128)(2,1)S(1)} %all_gather.3.refs_0_, bf16[896,128]{1,0:T(8,128)(2,1)S(1)} %collective-permute-done.refs_1_, bf16[896,128]{1,0:T(8,128)(2,1)S(1)} %collective-permute-done.1.refs_2_, ...), custom_call_target="tpu_custom_call", output_to_operand_aliasing={{}: (6, {})} | custom-call | flops 1879048192 | bytes 1048576 | tf_op jit(solution)/shard_map/pallas_call | solution.py:269
  67.7 0.0 collective-permute-done.9.refs_4_.refs_10_
  67.7 2.2 %collective-permute-start.10 = (bf16[8,64,256]{2,1,0:T(8,128)(2,1)S(1)}, bf16[8,64,256]{2,1,0:T(8,128)(2,1)S(1)}, u32[]{:S(2)}, u32[]{:S(2)}) collective-permute-start(bf16[8,64,256]{2,1,0:T(8,128)(2,1)S(1)} %collective-permute-done.9.refs_4_.refs_10_), channel_id=1, source_target_pairs={{0,2},{2,4},{4,6},{6,256},{256,258},{258,260},{260,262},{262,0},{1... | collective-permute-start | bytes 786440 | tf_op jit(solution)/shard_map/ppermute | solution.py:235
  69.9 2.9 %shard_map.41.refs_5_ = f32[3584,256]{1,0:T(8,128)S(1)} custom-call(s32[5]{0:T(128)S(1)} %stack.23.at_ref.at, bf16[896,128]{1,0:T(8,128)(2,1)S(1)} %all_gather.3.refs_0_, bf16[896,128]{1,0:T(8,128)(2,1)S(1)} %collective-permute-done.refs_1_, bf16[896,128]{1,0:T(8,128)(2,1)S(1)} %collective-permute-done.1.refs_2_, ...), custom_call_target="tpu_custom_call", output_to_operand_aliasing={{}: (6, {})} | custom-call | flops 1879048192 | bytes 1048576 | tf_op jit(solution)/shard_map/pallas_call | solution.py:269
  72.8 0.0 collective-permute-done.5.refs_4_.refs_7_
  72.9 1.9 %collective-permute-start.6 = (bf16[8,64,256]{2,1,0:T(8,128)(2,1)S(1)}, bf16[8,64,256]{2,1,0:T(8,128)(2,1)S(1)}, u32[]{:S(2)}, u32[]{:S(2)}) collective-permute-start(bf16[8,64,256]{2,1,0:T(8,128)(2,1)S(1)} %collective-permute-done.5.refs_4_.refs_7_), channel_id=1, source_target_pairs={{0,2},{2,4},{4,6},{6,256},{256,258},{258,260},{260,262},{262,0},{1... | collective-permute-start | bytes 786440 | tf_op jit(solution)/shard_map/ppermute | solution.py:235
  74.8 2.8 %shard_map.42.refs_5_ = f32[3584,256]{1,0:T(8,128)S(1)} custom-call(s32[5]{0:T(128)S(1)} %stack.23.at_ref.at, bf16[896,128]{1,0:T(8,128)(2,1)S(1)} %all_gather.3.refs_0_, bf16[896,128]{1,0:T(8,128)(2,1)S(1)} %collective-permute-done.refs_1_, bf16[896,128]{1,0:T(8,128)(2,1)S(1)} %collective-permute-done.1.refs_2_, ...), custom_call_target="tpu_custom_call", output_to_operand_aliasing={{}: (6, {})} | custom-call | flops 1879048192 | bytes 1048576 | tf_op jit(solution)/shard_map/pallas_call | solution.py:269
  77.6 2.8 %shard_map.43.refs_12_ = f32[3584,256]{1,0:T(8,128)S(1)} custom-call(s32[5]{0:T(128)S(1)} %stack.23.at_ref.at, bf16[896,128]{1,0:T(8,128)(2,1)S(1)} %all_gather.3.refs_0_, bf16[896,128]{1,0:T(8,128)(2,1)S(1)} %collective-permute-done.refs_1_, bf16[896,128]{1,0:T(8,128)(2,1)S(1)} %collective-permute-done.1.refs_2_, ...), custom_call_target="tpu_custom_call", output_to_operand_aliasing={{}: (6, {})} | custom-call | flops 1879048192 | bytes 1048576 | tf_op jit(solution)/shard_map/pallas_call | solution.py:269
  80.3 0.0 copy-start
  80.3 1.5 %close.1 = bf16[8,480,128]{2,1,0:T(8,128)(2,1)S(1)} custom-call(s32[5]{0:T(128)S(1)} %stack.23.at_ref.at, bf16[896,128]{1,0:T(8,128)(2,1)S(1)} %all_gather.3.refs_0_, bf16[896,128]{1,0:T(8,128)(2,1)S(1)} %collective-permute-done.refs_1_, bf16[896,128]{1,0:T(8,128)(2,1)S(1)} %collective-permute-done.1.refs_2_, ...), custom_call_target="tpu_custom_call" | custom-call | flops 1879048192 | bytes 1048576 | tf_op jit(solution)/shard_map/close/pallas_call | solution.py:279
  81.8 18.7 %all_to_all.11.got_ref = bf16[8,480,128]{2,1,0:T(8,128)(2,1)S(1)} all-to-all(bf16[8,480,128]{2,1,0:T(8,128)(2,1)S(1)} %close.1), channel_id=1, replica_groups=mesh['zh'=2,'y'=8,'x'=4,'zl'=4,'c'=2] {'x','c'}, dimensions={0} | all-to-all | bytes 1966080 | tf_op jit(solution)/shard_map/all_to_all | solution.py:289
  100.5 2.5 %combine.1 = bf16[448,128]{1,0:T(8,128)(2,1)} custom-call(s32[5]{0:T(128)S(1)} %stack.23.at_ref.at, bf16[448,128]{1,0:T(8,128)(2,1)S(1)} %bitcast.8, bf16[8,480,128]{2,1,0:T(8,128)(2,1)S(1)} %all_to_all.11.got_ref), custom_call_target="tpu_custom_call" | custom-call | tf_op jit(solution)/shard_map/combine/pallas_call | solution.py:290
  (7 shorter events, 0.0 us)
Async XLA Ops:
  17.7 28.1 %collective-permute-start.7 = (bf16[8,64,256]{2,1,0:T(8,128)(2,1)S(1)}, bf16[8,64,256]{2,1,0:T(8,128)(2,1)S(1)}, u32[]{:S(2)}, u32[]{:S(2)}) collective-permute-start(bf16[8,64,256]{2,1,0:T(8,128)(2,1)S(1)} %all_to_all.10.refs_4_), channel_id=1, source_target_pairs={{0,1},{1,0},{2,3},{3,2},{4,5},{5,4},{6,7},{7,6},{8,9},{9,8},{10,11... | collective-permute-start | bytes 786440 | tf_op jit(solution)/shard_map/ppermute | solution.py:261
  25.1 22.9 %collective-permute-start = (bf16[896,128]{1,0:T(8,128)(2,1)S(1)}, bf16[896,128]{1,0:T(8,128)(2,1)S(1)}, u32[]{:S(2)}, u32[]{:S(2)}) collective-permute-start(bf16[896,128]{1,0:T(8,128)(2,1)S(1)} %all_gather.3.refs_0_), channel_id=1, source_target_pairs={{0,8},{8,16},{16,24},{24,0},{1,9},{9,17},{17,25},{25,1},{2,10},{10... | collective-permute-start | bytes 688136 | tf_op jit(solution)/shard_map/ppermute | solution.py:239
  28.2 19.8 %collective-permute-start.1 = (bf16[896,128]{1,0:T(8,128)(2,1)S(1)}, bf16[896,128]{1,0:T(8,128)(2,1)S(1)}, u32[]{:S(2)}, u32[]{:S(2)}) collective-permute-start(bf16[896,128]{1,0:T(8,128)(2,1)S(1)} %all_gather.3.refs_0_), channel_id=1, source_target_pairs={{0,24},{8,0},{16,8},{24,16},{1,25},{9,1},{17,9},{25,17},{2,26},{10... | collective-permute-start | bytes 688136 | tf_op jit(solution)/shard_map/ppermute | solution.py:239
  31.6 16.4 %collective-permute-start.2 = (bf16[896,128]{1,0:T(8,128)(2,1)S(1)}, bf16[896,128]{1,0:T(8,128)(2,1)S(1)}, u32[]{:S(2)}, u32[]{:S(2)}) collective-permute-start(bf16[896,128]{1,0:T(8,128)(2,1)S(1)} %all_gather.3.refs_0_), channel_id=1, source_target_pairs={{0,16},{8,24},{16,0},{24,8},{1,17},{9,25},{17,1},{25,9},{2,18},{10... | collective-permute-start | bytes 688136 | tf_op jit(solution)/shard_map/ppermute | solution.py:239
  35.1 15.9 %collective-permute-start.3 = (bf16[8,64,256]{2,1,0:T(8,128)(2,1)S(1)}, bf16[8,64,256]{2,1,0:T(8,128)(2,1)S(1)}, u32[]{:S(2)}, u32[]{:S(2)}) collective-permute-start(bf16[8,64,256]{2,1,0:T(8,128)(2,1)S(1)} %all_to_all.10.refs_4_), channel_id=1, source_target_pairs={{0,2},{2,4},{4,6},{6,256},{256,258},{258,260},{260,262},{262,0},{1... | collective-permute-start | bytes 786440 | tf_op jit(solution)/shard_map/ppermute | solution.py:235
  45.8 11.9 %collective-permute-start.8 = (bf16[8,64,256]{2,1,0:T(8,128)(2,1)S(1)}, bf16[8,64,256]{2,1,0:T(8,128)(2,1)S(1)}, u32[]{:S(2)}, u32[]{:S(2)}) collective-permute-start(bf16[8,64,256]{2,1,0:T(8,128)(2,1)S(1)} %collective-permute-done.7), channel_id=1, source_target_pairs={{0,2},{2,4},{4,6},{6,256},{256,258},{258,260},{260,262},{262,0},{1... | collective-permute-start | bytes 786440 | tf_op jit(solution)/shard_map/ppermute | solution.py:235
  50.9 11.8 %collective-permute-start.4 = (bf16[8,64,256]{2,1,0:T(8,128)(2,1)S(1)}, bf16[8,64,256]{2,1,0:T(8,128)(2,1)S(1)}, u32[]{:S(2)}, u32[]{:S(2)}) collective-permute-start(bf16[8,64,256]{2,1,0:T(8,128)(2,1)S(1)} %collective-permute-done.3.refs_4_.refs_5_), channel_id=1, source_target_pairs={{0,2},{2,4},{4,6},{6,256},{256,258},{258,260},{260,262},{262,0},{1... | collective-permute-start | bytes 786440 | tf_op jit(solution)/shard_map/ppermute | solution.py:235
  57.8 9.9 %collective-permute-start.9 = (bf16[8,64,256]{2,1,0:T(8,128)(2,1)S(1)}, bf16[8,64,256]{2,1,0:T(8,128)(2,1)S(1)}, u32[]{:S(2)}, u32[]{:S(2)}) collective-permute-start(bf16[8,64,256]{2,1,0:T(8,128)(2,1)S(1)} %collective-permute-done.8.refs_4_.refs_9_), channel_id=1, source_target_pairs={{0,2},{2,4},{4,6},{6,256},{256,258},{258,260},{260,262},{262,0},{1... | collective-permute-start | bytes 786440 | tf_op jit(solution)/shard_map/ppermute | solution.py:235
  62.8 10.1 %collective-permute-start.5 = (bf16[8,64,256]{2,1,0:T(8,128)(2,1)S(1)}, bf16[8,64,256]{2,1,0:T(8,128)(2,1)S(1)}, u32[]{:S(2)}, u32[]{:S(2)}) collective-permute-start(bf16[8,64,256]{2,1,0:T(8,128)(2,1)S(1)} %collective-permute-done.4.refs_4_.refs_6_), channel_id=1, source_target_pairs={{0,2},{2,4},{4,6},{6,256},{256,258},{258,260},{260,262},{262,0},{1... | collective-permute-start | bytes 786440 | tf_op jit(solution)/shard_map/ppermute | solution.py:235
  67.7 9.8 %collective-permute-start.10 = (bf16[8,64,256]{2,1,0:T(8,128)(2,1)S(1)}, bf16[8,64,256]{2,1,0:T(8,128)(2,1)S(1)}, u32[]{:S(2)}, u32[]{:S(2)}) collective-permute-start(bf16[8,64,256]{2,1,0:T(8,128)(2,1)S(1)} %collective-permute-done.9.refs_4_.refs_10_), channel_id=1, source_target_pairs={{0,2},{2,4},{4,6},{6,256},{256,258},{258,260},{260,262},{262,0},{1... | collective-permute-start | bytes 786440 | tf_op jit(solution)/shard_map/ppermute | solution.py:235
  72.9 7.5 %collective-permute-start.6 = (bf16[8,64,256]{2,1,0:T(8,128)(2,1)S(1)}, bf16[8,64,256]{2,1,0:T(8,128)(2,1)S(1)}, u32[]{:S(2)}, u32[]{:S(2)}) collective-permute-start(bf16[8,64,256]{2,1,0:T(8,128)(2,1)S(1)} %collective-permute-done.5.refs_4_.refs_7_), channel_id=1, source_target_pairs={{0,2},{2,4},{4,6},{6,256},{256,258},{258,260},{260,262},{262,0},{1... | collective-permute-start | bytes 786440 | tf_op jit(solution)/shard_map/ppermute | solution.py:235
  80.3 20.2 %copy-start = (bf16[7,64,128]{2,1,0:T(8,128)(2,1)S(1)}, bf16[7,64,128]{2,1,0:T(8,128)(2,1)}, u32[]{:S(2)}) copy-start(bf16[7,64,128]{2,1,0:T(8,128)(2,1)} %param.3) | copy-start | bytes 344068

commit v3 on v2

--- a/solution.py
+++ b/solution.py
@@ -95,7 +95,7 @@
     return ref[lane, pl.ds(ys, 4), :, HEAD:].reshape(256, HEAD)
 
 
-def fold_piece(at, q_refs, sum_ref, kv_ref, zk, lane):
+def fold_piece(at, q_refs, sum_ref, kv_ref, zk, lane, first=False):
     @pl.when(zk // 4 <= at[0])
     def _():
         k = kv_ref[:, :, :HEAD].reshape(512, HEAD)
@@ -104,22 +104,21 @@
         for mate in range(MATES):
             weights = jnp.exp2(scores_of(queries_of(q_refs, mate), k))
             weights = keep(key_pos <= query_positions(at, mate), weights, 0.0)
-            sum_ref[rows_of(mate), :] += mix(weights, v)
-
-
-def step_kernel(hops, other, at_ref, *refs):
+            sums = mix(weights, v)
+            sum_ref[rows_of(mate), :] = sums if first else sum_ref[rows_of(mate), :] + sums
+
+
+def step_kernel(hops, other, *refs):
     q_refs, kv_ref, sum_ref = refs[:4], refs[4], refs[-1]
-    at = zh, y, x, zl, c = tuple(at_ref[i] for i in range(5))
-    if hops == 0:
-        sum_ref[...] = jnp.zeros(sum_ref.shape, f32)
+    at = zh, y, x, zl, c = place()
     zk = (zh * 4 + zl + jnp.where(c == 0, 8 - hops, hops)) % 8
-    fold_piece(at, q_refs, sum_ref, kv_ref, zk, 1 - c if other else c)
-
-
-def close_kernel(at_ref, *refs):
+    fold_piece(at, q_refs, sum_ref, kv_ref, zk, 1 - c if other else c, first=hops == 0)
+
+
+def close_kernel(*refs):
     q_refs, mines, others, (sum_ref, out_ref, kv_ref, q_copy) = refs[:4], refs[4:9], refs[9:12], refs[12:]
     far_ref = mines[4]
-    at = zh, y, x, zl, c = tuple(at_ref[i] for i in range(5))
+    at = zh, y, x, zl, c = place()
     z = zh * 4 + zl
     far = (z + 4) % 8
 
@@ -132,14 +131,20 @@
         lowest = jnp.minimum(lowest, (zk // 4 * 256 + x * 8 + zk % 4 * 2 + lane) * TOK)
     lowest = jnp.maximum(lowest, SINKS)
 
+    pick = lax.broadcasted_iota(jnp.int32, (16, HEAD), 0) == lax.broadcasted_iota(jnp.int32, (16, HEAD), 1)
+    pick = jnp.where(pick, 1.0, 0.0).astype(bf16)
+
     def finish(mate, peak):
         number = number_of(at, mate)
         out_ref[number, :ROWS, :] = sum_ref[rows_of(mate), :HEAD].astype(bf16)
         total = sum_ref[rows_of(mate), HEAD:]
         high = total.astype(bf16).astype(f32)
         stat = jnp.where(number_row == 0, peak, jnp.where(number_row == 1, high, total - high))
+        stat = jnp.where(number_row < 3, stat, 0.0)
         stat = jnp.concatenate([stat, jnp.zeros((TOK, HEAD), f32)], axis=0)
-        tiles = [stat[chunk * 128 : (chunk + 1) * 128].T[:4] for chunk in range(CHUNKS)]
+        stat = stat.astype(bf16)
+        turned = lax.dot_general(pick, stat, (((1,), (1,)), ((), ())), preferred_element_type=f32)
+        tiles = [turned[:4, chunk * 128 : (chunk + 1) * 128] for chunk in range(CHUNKS)]
         out_ref[number, STAT : STAT + 16, :] = jnp.concatenate(tiles, axis=0).astype(bf16)
 
     lost = jnp.zeros((TOK, HEAD), jnp.bool_)
@@ -197,8 +202,8 @@
         out_ref[mate, EXTRA:, :] = both
 
 
-def combine_kernel(at, q_ref, got_ref, out_ref):
-    zh, y, x, zl, c = (at[i] for i in range(5))
+def combine_kernel(q_ref, got_ref, out_ref):
+    zh, y, x, zl, c = place()
     first = ((zh * 8 + y) * 32 + x * 8 + zl * 2 + c) * TOK
     extra = got_ref[jnp.where(zh * 4 + zl <= 4, 0, 1), EXTRA:, :]
     values = extra.astype(f32)
@@ -245,7 +250,6 @@
 
 
 def per_device(queries, keys, values):
-    at = jnp.stack(place()).astype(jnp.int32)
     q = queries.reshape(ROWS, HEAD)
     q_own = lax.all_gather(q, "c", axis=0, tiled=True)
     kv = jnp.broadcast_to(jnp.concatenate([keys, values], axis=1)[None], (8, TOK, 2 * HEAD))
@@ -253,7 +257,6 @@
     q_all = [q_own]
     for hops in (1, -1, 2):
         q_all.append(along_x(q_own, hops))
-    smem = pl.BlockSpec(memory_space=pltpu.SMEM)
     vmem = pl.BlockSpec(memory_space=pltpu.VMEM)
     mines = [own]
     for _ in range(1, 5):
@@ -269,32 +272,32 @@
             pl.pallas_call(
                 functools.partial(step_kernel, hops, other),
                 out_shape=sums,
-                in_specs=[smem] + [vmem] * (5 + len(total)),
+                in_specs=[vmem] * (5 + len(total)),
                 out_specs=vmem,
-                input_output_aliases={6: 0} if total else {},
+                input_output_aliases={5: 0} if total else {},
                 cost_estimate=cost(512),
                 compiler_params=roomy,
-            )(at, *q_all, (others if other else mines)[hops], *total),
+            )(*q_all, (others if other else mines)[hops], *total),
         )
     partial = pl.pallas_call(
         close_kernel,
         out_shape=jax.ShapeDtypeStruct((MATES, PAYLOAD, HEAD), bf16),
-        in_specs=[smem] + [vmem] * 13,
+        in_specs=[vmem] * 13,
         out_specs=vmem,
         scratch_shapes=[pltpu.VMEM((5, 2, 8, TOK, 2 * HEAD), bf16), pltpu.VMEM((ALL_ROWS, HEAD), bf16)],
         cost_estimate=cost(512),
         compiler_params=roomy,
         name="close",
-    )(at, *q_all, *mines, *others[1:], *total)
+    )(*q_all, *mines, *others[1:], *total)
     got = lax.all_to_all(partial, TEAM, 0, 0, tiled=True)
     out = pl.pallas_call(
         combine_kernel,
         out_shape=jax.ShapeDtypeStruct((ROWS, HEAD), bf16),
-        in_specs=[smem, vmem, vmem],
+        in_specs=[vmem, vmem],
         out_specs=vmem,
         compiler_params=roomy,
         name="combine",
-    )(at, q, got)
+    )(q, got)
     return out.reshape(GROUP, TOK, HEAD)
 
 

time: 104 us -> 101 us (0.971)
  Pallas kernels: 23.5 us -> 18.5 us
  blocking collectives: 37.8 us -> 39.6 us
    pallas_call x7, Pallas kernels: 19.6 us -> 15.7 us  [per_device(): pl.pallas_call(functools.partial(step_kernel, hops, other), out_shape=sum...]
    all_to_all x1, blocking collectives: 18.7 us -> 20.4 us  [per_device(): got = lax.all_to_all(partial, TEAM, 0, 0, tiled=True)]
  transfers between devices with their start and end apart: 11 -> 11, of which waited for: 0 -> 1; matrix products, arithmetic and copies ran while one was open for 0% -> 0% of each run, Pallas kernels for 19% -> 16%
where the time goes in v3:
time: 101 us
  starting transfers between devices  40.6 us (40%)
  blocking collectives  39.6 us (39%)
  Pallas kernels  18.5 us (18%)
  waiting for transfers between devices  1.04 us (1%)
    ppermute x7, starting transfers between devices, onward(): return lax.ppermute(piece, (*Z, 'c'), pairs)  25.4 us
    all_to_all x1, blocking collectives, per_device(): got = lax.all_to_all(partial, TEAM, 0, 0, tiled=True)  20.4 us
    all_to_all x1, blocking collectives, per_device(): own = lax.all_to_all(kv, 'y', 0, 0, tiled=True)  17 us
    pallas_call x7, Pallas kernels, per_device(): pl.pallas_call(functools.partial(step_kernel, hops, other), out_shape=sum...  15.7 us
    ppermute x3, starting transfers between devices, along_x(): return lax.ppermute(block, 'x', [(n, (n + hops) % 4) for n in range(4)])  9.92 us
    ppermute x1, starting transfers between devices, per_device(): others = [lax.ppermute(own, 'c', [(0, 1), (1, 0)])]  5.19 us
    all_gather x1, blocking collectives, per_device(): q_own = lax.all_gather(q, 'c', axis=0, tiled=True)  2.18 us
  transfers between devices with their start and end apart: 11, of which 1 were waited for; matrix products, arithmetic and copies ran while one was open for 0% of the time, Pallas kernels for 16%

profile of v3, /device:TPU:1, one launch (start us, length us, event | category | flops | bytes accessed | tf_op | source)
XLA Modules:
  0.0 100.7 jit_solution(13958783266536274813)
XLA Ops:
  0.0 0.7 pad_maximum_fusion
  0.8 17.0 %all_to_all.10.refs_4_ = bf16[8,64,256]{2,1,0:T(8,128)(2,1)S(1)} all-to-all(bf16[8,64,256]{2,1,0:T(8,128)(2,1)S(1)} %broadcast_in_dim.2), channel_id=1, replica_groups=mesh['zh'=2,'y'=8,'x'=4,'zl'=4,'c'=2] {'y'}, dimensions={0} | all-to-all | bytes 524288 | tf_op jit(solution)/shard_map/all_to_all | solution.py:256
  17.7 5.2 %collective-permute-start.7 = (bf16[8,64,256]{2,1,0:T(8,128)(2,1)S(1)}, bf16[8,64,256]{2,1,0:T(8,128)(2,1)S(1)}, u32[]{:S(2)}, u32[]{:S(2)}) collective-permute-start(bf16[8,64,256]{2,1,0:T(8,128)(2,1)S(1)} %all_to_all.10.refs_4_), channel_id=1, source_target_pairs={{0,1},{1,0},{2,3},{3,2},{4,5},{5,4},{6,7},{7,6},{8,9},{9,8},{10,11... | collective-permute-start | bytes 786440 | tf_op jit(solution)/shard_map/ppermute | solution.py:264
  22.9 2.2 %all_gather.3.refs_0_ = bf16[896,128]{1,0:T(8,128)(2,1)S(1)} all-gather(bf16[448,128]{1,0:T(8,128)(2,1)} %bitcast.2), channel_id=1, replica_groups=mesh['zh'=2,'y'=8,'x'=4,'zl'=4,'c'=2] {'c'}, dimensions={0}, use_global_device_ids=true | all-gather | bytes 344064 | tf_op jit(solution)/shard_map/all_gather | solution.py:254
  25.1 3.1 %collective-permute-start = (bf16[896,128]{1,0:T(8,128)(2,1)S(1)}, bf16[896,128]{1,0:T(8,128)(2,1)S(1)}, u32[]{:S(2)}, u32[]{:S(2)}) collective-permute-start(bf16[896,128]{1,0:T(8,128)(2,1)S(1)} %all_gather.3.refs_0_), channel_id=1, source_target_pairs={{0,8},{8,16},{16,24},{24,0},{1,9},{9,17},{17,25},{25,1},{2,10},{10... | collective-permute-start | bytes 688136 | tf_op jit(solution)/shard_map/ppermute | solution.py:244
  28.2 3.4 %collective-permute-start.1 = (bf16[896,128]{1,0:T(8,128)(2,1)S(1)}, bf16[896,128]{1,0:T(8,128)(2,1)S(1)}, u32[]{:S(2)}, u32[]{:S(2)}) collective-permute-start(bf16[896,128]{1,0:T(8,128)(2,1)S(1)} %all_gather.3.refs_0_), channel_id=1, source_target_pairs={{0,24},{8,0},{16,8},{24,16},{1,25},{9,1},{17,9},{25,17},{2,26},{10... | collective-permute-start | bytes 688136 | tf_op jit(solution)/shard_map/ppermute | solution.py:244
  31.6 3.4 %collective-permute-start.2 = (bf16[896,128]{1,0:T(8,128)(2,1)S(1)}, bf16[896,128]{1,0:T(8,128)(2,1)S(1)}, u32[]{:S(2)}, u32[]{:S(2)}) collective-permute-start(bf16[896,128]{1,0:T(8,128)(2,1)S(1)} %all_gather.3.refs_0_), channel_id=1, source_target_pairs={{0,16},{8,24},{16,0},{24,8},{1,17},{9,25},{17,1},{25,9},{2,18},{10... | collective-permute-start | bytes 688136 | tf_op jit(solution)/shard_map/ppermute | solution.py:244
  35.1 10.7 %collective-permute-start.3 = (bf16[8,64,256]{2,1,0:T(8,128)(2,1)S(1)}, bf16[8,64,256]{2,1,0:T(8,128)(2,1)S(1)}, u32[]{:S(2)}, u32[]{:S(2)}) collective-permute-start(bf16[8,64,256]{2,1,0:T(8,128)(2,1)S(1)} %all_to_all.10.refs_4_), channel_id=1, source_target_pairs={{0,2},{2,4},{4,6},{6,256},{256,258},{258,260},{260,262},{262,0},{1... | collective-permute-start | bytes 786440 | tf_op jit(solution)/shard_map/ppermute | solution.py:240
  45.7 0.0 collective-permute-done.7
  45.8 2.2 %collective-permute-start.8 = (bf16[8,64,256]{2,1,0:T(8,128)(2,1)S(1)}, bf16[8,64,256]{2,1,0:T(8,128)(2,1)S(1)}, u32[]{:S(2)}, u32[]{:S(2)}) collective-permute-start(bf16[8,64,256]{2,1,0:T(8,128)(2,1)S(1)} %collective-permute-done.7), channel_id=1, source_target_pairs={{0,2},{2,4},{4,6},{6,256},{256,258},{258,260},{260,262},{262,0},{1... | collective-permute-start | bytes 786440 | tf_op jit(solution)/shard_map/ppermute | solution.py:240
  47.9 0.0 collective-permute-done.refs_1_
  48.0 0.0 collective-permute-done.1.refs_2_
  48.0 0.0 collective-permute-done.2.refs_3_
  48.0 2.2 %shard_map.37.refs_5_ = f32[3584,256]{1,0:T(8,128)S(1)} custom-call(bf16[896,128]{1,0:T(8,128)(2,1)S(1)} %all_gather.3.refs_0_, bf16[896,128]{1,0:T(8,128)(2,1)S(1)} %collective-permute-done.refs_1_, bf16[896,128]{1,0:T(8,128)(2,1)S(1)} %collective-permute-done.1.refs_2_, bf16[896,128]{1,0:T(8,128)(2,1)S(1)} %collective-permute-done.2.refs_3_, ...), custom_call_target="tpu_custom_call" | custom-call | flops 1879048192 | bytes 1048576 | tf_op jit(solution)/shard_map/pallas_call | solution.py:272
  50.2 4.1 %collective-permute-start.4 = (bf16[8,64,256]{2,1,0:T(8,128)(2,1)S(1)}, bf16[8,64,256]{2,1,0:T(8,128)(2,1)S(1)}, u32[]{:S(2)}, u32[]{:S(2)}) collective-permute-start(bf16[8,64,256]{2,1,0:T(8,128)(2,1)S(1)} %collective-permute-done.3.refs_4_.refs_5_), channel_id=1, source_target_pairs={{0,2},{2,4},{4,6},{6,256},{256,258},{258,260},{260,262},{262,0},{1... | collective-permute-start | bytes 786440 | tf_op jit(solution)/shard_map/ppermute | solution.py:240
  54.3 2.2 %shard_map.38.refs_5_ = f32[3584,256]{1,0:T(8,128)S(1)} custom-call(bf16[896,128]{1,0:T(8,128)(2,1)S(1)} %all_gather.3.refs_0_, bf16[896,128]{1,0:T(8,128)(2,1)S(1)} %collective-permute-done.refs_1_, bf16[896,128]{1,0:T(8,128)(2,1)S(1)} %collective-permute-done.1.refs_2_, ...), custom_call_target="tpu_custom_call", output_to_operand_aliasing={{}: (5, {})} | custom-call | flops 1879048192 | bytes 1048576 | tf_op jit(solution)/shard_map/pallas_call | solution.py:272
  56.6 2.2 %collective-permute-start.9 = (bf16[8,64,256]{2,1,0:T(8,128)(2,1)S(1)}, bf16[8,64,256]{2,1,0:T(8,128)(2,1)S(1)}, u32[]{:S(2)}, u32[]{:S(2)}) collective-permute-start(bf16[8,64,256]{2,1,0:T(8,128)(2,1)S(1)} %collective-permute-done.8.refs_4_.refs_9_), channel_id=1, source_target_pairs={{0,2},{2,4},{4,6},{6,256},{256,258},{258,260},{260,262},{262,0},{1... | collective-permute-start | bytes 786440 | tf_op jit(solution)/shard_map/ppermute | solution.py:240
  58.8 2.2 %shard_map.39.refs_5_ = f32[3584,256]{1,0:T(8,128)S(1)} custom-call(bf16[896,128]{1,0:T(8,128)(2,1)S(1)} %all_gather.3.refs_0_, bf16[896,128]{1,0:T(8,128)(2,1)S(1)} %collective-permute-done.refs_1_, bf16[896,128]{1,0:T(8,128)(2,1)S(1)} %collective-permute-done.1.refs_2_, ...), custom_call_target="tpu_custom_call", output_to_operand_aliasing={{}: (5, {})} | custom-call | flops 1879048192 | bytes 1048576 | tf_op jit(solution)/shard_map/pallas_call | solution.py:272
  61.0 0.0 collective-permute-done.4.refs_4_.refs_6_
  61.0 2.2 %collective-permute-start.5 = (bf16[8,64,256]{2,1,0:T(8,128)(2,1)S(1)}, bf16[8,64,256]{2,1,0:T(8,128)(2,1)S(1)}, u32[]{:S(2)}, u32[]{:S(2)}) collective-permute-start(bf16[8,64,256]{2,1,0:T(8,128)(2,1)S(1)} %collective-permute-done.4.refs_4_.refs_6_), channel_id=1, source_target_pairs={{0,2},{2,4},{4,6},{6,256},{256,258},{258,260},{260,262},{262,0},{1... | collective-permute-start | bytes 786440 | tf_op jit(solution)/shard_map/ppermute | solution.py:240
  63.2 2.2 %shard_map.40.refs_5_ = f32[3584,256]{1,0:T(8,128)S(1)} custom-call(bf16[896,128]{1,0:T(8,128)(2,1)S(1)} %all_gather.3.refs_0_, bf16[896,128]{1,0:T(8,128)(2,1)S(1)} %collective-permute-done.refs_1_, bf16[896,128]{1,0:T(8,128)(2,1)S(1)} %collective-permute-done.1.refs_2_, ...), custom_call_target="tpu_custom_call", output_to_operand_aliasing={{}: (5, {})} | custom-call | flops 1879048192 | bytes 1048576 | tf_op jit(solution)/shard_map/pallas_call | solution.py:272
  65.4 0.0 collective-permute-done.9.refs_4_.refs_10_
  65.4 2.2 %collective-permute-start.10 = (bf16[8,64,256]{2,1,0:T(8,128)(2,1)S(1)}, bf16[8,64,256]{2,1,0:T(8,128)(2,1)S(1)}, u32[]{:S(2)}, u32[]{:S(2)}) collective-permute-start(bf16[8,64,256]{2,1,0:T(8,128)(2,1)S(1)} %collective-permute-done.9.refs_4_.refs_10_), channel_id=1, source_target_pairs={{0,2},{2,4},{4,6},{6,256},{256,258},{258,260},{260,262},{262,0},{1... | collective-permute-start | bytes 786440 | tf_op jit(solution)/shard_map/ppermute | solution.py:240
  67.6 2.4 %shard_map.41.refs_5_ = f32[3584,256]{1,0:T(8,128)S(1)} custom-call(bf16[896,128]{1,0:T(8,128)(2,1)S(1)} %all_gather.3.refs_0_, bf16[896,128]{1,0:T(8,128)(2,1)S(1)} %collective-permute-done.refs_1_, bf16[896,128]{1,0:T(8,128)(2,1)S(1)} %collective-permute-done.1.refs_2_, ...), custom_call_target="tpu_custom_call", output_to_operand_aliasing={{}: (5, {})} | custom-call | flops 1879048192 | bytes 1048576 | tf_op jit(solution)/shard_map/pallas_call | solution.py:272
  70.0 1.9 %collective-permute-start.6 = (bf16[8,64,256]{2,1,0:T(8,128)(2,1)S(1)}, bf16[8,64,256]{2,1,0:T(8,128)(2,1)S(1)}, u32[]{:S(2)}, u32[]{:S(2)}) collective-permute-start(bf16[8,64,256]{2,1,0:T(8,128)(2,1)S(1)} %collective-permute-done.5.refs_4_.refs_7_), channel_id=1, source_target_pairs={{0,2},{2,4},{4,6},{6,256},{256,258},{258,260},{260,262},{262,0},{1... | collective-permute-start | bytes 786440 | tf_op jit(solution)/shard_map/ppermute | solution.py:240
  71.9 2.2 %shard_map.42.refs_5_ = f32[3584,256]{1,0:T(8,128)S(1)} custom-call(bf16[896,128]{1,0:T(8,128)(2,1)S(1)} %all_gather.3.refs_0_, bf16[896,128]{1,0:T(8,128)(2,1)S(1)} %collective-permute-done.refs_1_, bf16[896,128]{1,0:T(8,128)(2,1)S(1)} %collective-permute-done.1.refs_2_, ...), custom_call_target="tpu_custom_call", output_to_operand_aliasing={{}: (5, {})} | custom-call | flops 1879048192 | bytes 1048576 | tf_op jit(solution)/shard_map/pallas_call | solution.py:272
  74.2 2.2 %shard_map.43.refs_12_ = f32[3584,256]{1,0:T(8,128)S(1)} custom-call(bf16[896,128]{1,0:T(8,128)(2,1)S(1)} %all_gather.3.refs_0_, bf16[896,128]{1,0:T(8,128)(2,1)S(1)} %collective-permute-done.refs_1_, bf16[896,128]{1,0:T(8,128)(2,1)S(1)} %collective-permute-done.1.refs_2_, ...), custom_call_target="tpu_custom_call", output_to_operand_aliasing={{}: (5, {})} | custom-call | flops 1879048192 | bytes 1048576 | tf_op jit(solution)/shard_map/pallas_call | solution.py:272
  76.4 0.0 copy-start
  76.4 1.0 %collective-permute-done.6.refs_8_ = bf16[8,64,256]{2,1,0:T(8,128)(2,1)S(1)} collective-permute-done((bf16[8,64,256]{2,1,0:T(8,128)(2,1)S(1)}, bf16[8,64,256]{2,1,0:T(8,128)(2,1)S(1)}, u32[]{:S(2)}, u32[]{:S(2)}) %collective-permute-start.6) | collective-permute-done | bytes 262176 | tf_op jit(solution)/shard_map/ppermute | solution.py:240
  77.4 1.0 close.1
  78.4 20.4 %all_to_all.11.got_ref = bf16[8,480,128]{2,1,0:T(8,128)(2,1)S(1)} all-to-all(bf16[8,480,128]{2,1,0:T(8,128)(2,1)S(1)} %close.1), channel_id=1, replica_groups=mesh['zh'=2,'y'=8,'x'=4,'zl'=4,'c'=2] {'x','c'}, dimensions={0} | all-to-all | bytes 1966080 | tf_op jit(solution)/shard_map/all_to_all | solution.py:292
  98.8 1.9 %combine.1 = bf16[448,128]{1,0:T(8,128)(2,1)} custom-call(bf16[448,128]{1,0:T(8,128)(2,1)S(1)} %bitcast.3, bf16[8,480,128]{2,1,0:T(8,128)(2,1)S(1)} %all_to_all.11.got_ref), custom_call_target="tpu_custom_call" | custom-call | tf_op jit(solution)/shard_map/combine/pallas_call | solution.py:293
  (6 shorter events, 0.0 us)
Async XLA Ops:
  17.7 28.0 %collective-permute-start.7 = (bf16[8,64,256]{2,1,0:T(8,128)(2,1)S(1)}, bf16[8,64,256]{2,1,0:T(8,128)(2,1)S(1)}, u32[]{:S(2)}, u32[]{:S(2)}) collective-permute-start(bf16[8,64,256]{2,1,0:T(8,128)(2,1)S(1)} %all_to_all.10.refs_4_), channel_id=1, source_target_pairs={{0,1},{1,0},{2,3},{3,2},{4,5},{5,4},{6,7},{7,6},{8,9},{9,8},{10,11... | collective-permute-start | bytes 786440 | tf_op jit(solution)/shard_map/ppermute | solution.py:264
  25.1 22.8 %collective-permute-start = (bf16[896,128]{1,0:T(8,128)(2,1)S(1)}, bf16[896,128]{1,0:T(8,128)(2,1)S(1)}, u32[]{:S(2)}, u32[]{:S(2)}) collective-permute-start(bf16[896,128]{1,0:T(8,128)(2,1)S(1)} %all_gather.3.refs_0_), channel_id=1, source_target_pairs={{0,8},{8,16},{16,24},{24,0},{1,9},{9,17},{17,25},{25,1},{2,10},{10... | collective-permute-start | bytes 688136 | tf_op jit(solution)/shard_map/ppermute | solution.py:244
  28.2 19.7 %collective-permute-start.1 = (bf16[896,128]{1,0:T(8,128)(2,1)S(1)}, bf16[896,128]{1,0:T(8,128)(2,1)S(1)}, u32[]{:S(2)}, u32[]{:S(2)}) collective-permute-start(bf16[896,128]{1,0:T(8,128)(2,1)S(1)} %all_gather.3.refs_0_), channel_id=1, source_target_pairs={{0,24},{8,0},{16,8},{24,16},{1,25},{9,1},{17,9},{25,17},{2,26},{10... | collective-permute-start | bytes 688136 | tf_op jit(solution)/shard_map/ppermute | solution.py:244
  31.6 16.3 %collective-permute-start.2 = (bf16[896,128]{1,0:T(8,128)(2,1)S(1)}, bf16[896,128]{1,0:T(8,128)(2,1)S(1)}, u32[]{:S(2)}, u32[]{:S(2)}) collective-permute-start(bf16[896,128]{1,0:T(8,128)(2,1)S(1)} %all_gather.3.refs_0_), channel_id=1, source_target_pairs={{0,16},{8,24},{16,0},{24,8},{1,17},{9,25},{17,1},{25,9},{2,18},{10... | collective-permute-start | bytes 688136 | tf_op jit(solution)/shard_map/ppermute | solution.py:244
  35.1 15.1 %collective-permute-start.3 = (bf16[8,64,256]{2,1,0:T(8,128)(2,1)S(1)}, bf16[8,64,256]{2,1,0:T(8,128)(2,1)S(1)}, u32[]{:S(2)}, u32[]{:S(2)}) collective-permute-start(bf16[8,64,256]{2,1,0:T(8,128)(2,1)S(1)} %all_to_all.10.refs_4_), channel_id=1, source_target_pairs={{0,2},{2,4},{4,6},{6,256},{256,258},{258,260},{260,262},{262,0},{1... | collective-permute-start | bytes 786440 | tf_op jit(solution)/shard_map/ppermute | solution.py:240
  45.8 10.8 %collective-permute-start.8 = (bf16[8,64,256]{2,1,0:T(8,128)(2,1)S(1)}, bf16[8,64,256]{2,1,0:T(8,128)(2,1)S(1)}, u32[]{:S(2)}, u32[]{:S(2)}) collective-permute-start(bf16[8,64,256]{2,1,0:T(8,128)(2,1)S(1)} %collective-permute-done.7), channel_id=1, source_target_pairs={{0,2},{2,4},{4,6},{6,256},{256,258},{258,260},{260,262},{262,0},{1... | collective-permute-start | bytes 786440 | tf_op jit(solution)/shard_map/ppermute | solution.py:240
  50.2 10.8 %collective-permute-start.4 = (bf16[8,64,256]{2,1,0:T(8,128)(2,1)S(1)}, bf16[8,64,256]{2,1,0:T(8,128)(2,1)S(1)}, u32[]{:S(2)}, u32[]{:S(2)}) collective-permute-start(bf16[8,64,256]{2,1,0:T(8,128)(2,1)S(1)} %collective-permute-done.3.refs_4_.refs_5_), channel_id=1, source_target_pairs={{0,2},{2,4},{4,6},{6,256},{256,258},{258,260},{260,262},{262,0},{1... | collective-permute-start | bytes 786440 | tf_op jit(solution)/shard_map/ppermute | solution.py:240
  56.6 8.8 %collective-permute-start.9 = (bf16[8,64,256]{2,1,0:T(8,128)(2,1)S(1)}, bf16[8,64,256]{2,1,0:T(8,128)(2,1)S(1)}, u32[]{:S(2)}, u32[]{:S(2)}) collective-permute-start(bf16[8,64,256]{2,1,0:T(8,128)(2,1)S(1)} %collective-permute-done.8.refs_4_.refs_9_), channel_id=1, source_target_pairs={{0,2},{2,4},{4,6},{6,256},{256,258},{258,260},{260,262},{262,0},{1... | collective-permute-start | bytes 786440 | tf_op jit(solution)/shard_map/ppermute | solution.py:240
  61.0 9.0 %collective-permute-start.5 = (bf16[8,64,256]{2,1,0:T(8,128)(2,1)S(1)}, bf16[8,64,256]{2,1,0:T(8,128)(2,1)S(1)}, u32[]{:S(2)}, u32[]{:S(2)}) collective-permute-start(bf16[8,64,256]{2,1,0:T(8,128)(2,1)S(1)} %collective-permute-done.4.refs_4_.refs_6_), channel_id=1, source_target_pairs={{0,2},{2,4},{4,6},{6,256},{256,258},{258,260},{260,262},{262,0},{1... | collective-permute-start | bytes 786440 | tf_op jit(solution)/shard_map/ppermute | solution.py:240
  65.4 8.8 %collective-permute-start.10 = (bf16[8,64,256]{2,1,0:T(8,128)(2,1)S(1)}, bf16[8,64,256]{2,1,0:T(8,128)(2,1)S(1)}, u32[]{:S(2)}, u32[]{:S(2)}) collective-permute-start(bf16[8,64,256]{2,1,0:T(8,128)(2,1)S(1)} %collective-permute-done.9.refs_4_.refs_10_), channel_id=1, source_target_pairs={{0,2},{2,4},{4,6},{6,256},{256,258},{258,260},{260,262},{262,0},{1... | collective-permute-start | bytes 786440 | tf_op jit(solution)/shard_map/ppermute | solution.py:240
  70.0 7.4 %collective-permute-start.6 = (bf16[8,64,256]{2,1,0:T(8,128)(2,1)S(1)}, bf16[8,64,256]{2,1,0:T(8,128)(2,1)S(1)}, u32[]{:S(2)}, u32[]{:S(2)}) collective-permute-start(bf16[8,64,256]{2,1,0:T(8,128)(2,1)S(1)} %collective-permute-done.5.refs_4_.refs_7_), channel_id=1, source_target_pairs={{0,2},{2,4},{4,6},{6,256},{256,258},{258,260},{260,262},{262,0},{1... | collective-permute-start | bytes 786440 | tf_op jit(solution)/shard_map/ppermute | solution.py:240
  76.4 22.4 %copy-start = (bf16[7,64,128]{2,1,0:T(8,128)(2,1)S(1)}, bf16[7,64,128]{2,1,0:T(8,128)(2,1)}, u32[]{:S(2)}) copy-start(bf16[7,64,128]{2,1,0:T(8,128)(2,1)} %param.3) | copy-start | bytes 344068

commit v4 on v3

--- a/solution.py
+++ b/solution.py
@@ -20,7 +20,7 @@
 TOK = 64
 ROWS = GROUP * TOK
 MATES = 8
-HOPS = (0, 3, 1, 2)
+HOPS = (0, 2, 3, 1)
 SEQ = 32768
 SINKS = 4
 ALL_ROWS = MATES * ROWS
@@ -53,7 +53,7 @@
 
 
 def number_of(at, mate):
-    hop = HOPS[mate // 2] if isinstance(mate, int) else jnp.where(mate < 2, 0, jnp.where(mate < 4, 3, jnp.where(mate < 6, 1, 2)))
+    hop = HOPS[mate // 2] if isinstance(mate, int) else jnp.where(mate < 2, 0, jnp.where(mate < 4, 2, jnp.where(mate < 6, 3, 1)))
     return (at[2] + hop) % 4 * 2 + mate % 2
 
 
@@ -255,7 +255,7 @@
     kv = jnp.broadcast_to(jnp.concatenate([keys, values], axis=1)[None], (8, TOK, 2 * HEAD))
     own = lax.all_to_all(kv, "y", 0, 0, tiled=True)
     q_all = [q_own]
-    for hops in (1, -1, 2):
+    for hops in (2, 1, -1):
         q_all.append(along_x(q_own, hops))
     vmem = pl.BlockSpec(memory_space=pltpu.VMEM)
     mines = [own]

time: 101 us -> 101 us (level)
  waiting for transfers between devices: 1.04 us -> 0.03 us
    ppermute x3, starting transfers between devices: 9.92 us -> 11.1 us  [along_x(): return lax.ppermute(block, 'x', [(n, (n + hops) % 4) for n in range(4)])]
    ppermute x7, waiting for transfers between devices: 1.03 us -> 0.02 us  [onward(): return lax.ppermute(piece, (*Z, 'c'), pairs)]
  transfers between devices with their start and end apart: 11 -> 11, of which waited for: 1 -> 0; matrix products, arithmetic and copies ran while one was open for 0% -> 0% of each run, Pallas kernels for 16% -> 16%
where the time goes in v4:
time: 101 us
  starting transfers between devices  41.5 us (41%)
  blocking collectives  39.5 us (39%)
  Pallas kernels  18.6 us (18%)
    ppermute x7, starting transfers between devices, onward(): return lax.ppermute(piece, (*Z, 'c'), pairs)  25.2 us
    all_to_all x1, blocking collectives, per_device(): got = lax.all_to_all(partial, TEAM, 0, 0, tiled=True)  20.3 us
    all_to_all x1, blocking collectives, per_device(): own = lax.all_to_all(kv, 'y', 0, 0, tiled=True)  17 us
    pallas_call x7, Pallas kernels, per_device(): pl.pallas_call(functools.partial(step_kernel, hops, other), out_shape=sum...  15.7 us
    ppermute x3, starting transfers between devices, along_x(): return lax.ppermute(block, 'x', [(n, (n + hops) % 4) for n in range(4)])  11.1 us
    ppermute x1, starting transfers between devices, per_device(): others = [lax.ppermute(own, 'c', [(0, 1), (1, 0)])]  5.19 us
    all_gather x1, blocking collectives, per_device(): q_own = lax.all_gather(q, 'c', axis=0, tiled=True)  2.18 us
  transfers between devices with their start and end apart: 11, of which 0 were waited for; matrix products, arithmetic and copies ran while one was open for 0% of the time, Pallas kernels for 16%

profile of v4, /device:TPU:1, one launch (start us, length us, event | category | flops | bytes accessed | tf_op | source)
XLA Modules:
  0.0 100.5 jit_solution(3406214797149261632)
XLA Ops:
  0.0 0.7 pad_maximum_fusion
  0.8 17.0 %all_to_all.10.refs_4_ = bf16[8,64,256]{2,1,0:T(8,128)(2,1)S(1)} all-to-all(bf16[8,64,256]{2,1,0:T(8,128)(2,1)S(1)} %broadcast_in_dim.2), channel_id=1, replica_groups=mesh['zh'=2,'y'=8,'x'=4,'zl'=4,'c'=2] {'y'}, dimensions={0} | all-to-all | bytes 524288 | tf_op jit(solution)/shard_map/all_to_all | solution.py:256
  17.7 5.2 %collective-permute-start.7 = (bf16[8,64,256]{2,1,0:T(8,128)(2,1)S(1)}, bf16[8,64,256]{2,1,0:T(8,128)(2,1)S(1)}, u32[]{:S(2)}, u32[]{:S(2)}) collective-permute-start(bf16[8,64,256]{2,1,0:T(8,128)(2,1)S(1)} %all_to_all.10.refs_4_), channel_id=1, source_target_pairs={{0,1},{1,0},{2,3},{3,2},{4,5},{5,4},{6,7},{7,6},{8,9},{9,8},{10,11... | collective-permute-start | bytes 786440 | tf_op jit(solution)/shard_map/ppermute | solution.py:264
  22.9 2.2 %all_gather.3.refs_0_ = bf16[896,128]{1,0:T(8,128)(2,1)S(1)} all-gather(bf16[448,128]{1,0:T(8,128)(2,1)} %bitcast.2), channel_id=1, replica_groups=mesh['zh'=2,'y'=8,'x'=4,'zl'=4,'c'=2] {'c'}, dimensions={0}, use_global_device_ids=true | all-gather | bytes 344064 | tf_op jit(solution)/shard_map/all_gather | solution.py:254
  25.1 4.6 %collective-permute-start = (bf16[896,128]{1,0:T(8,128)(2,1)S(1)}, bf16[896,128]{1,0:T(8,128)(2,1)S(1)}, u32[]{:S(2)}, u32[]{:S(2)}) collective-permute-start(bf16[896,128]{1,0:T(8,128)(2,1)S(1)} %all_gather.3.refs_0_), channel_id=1, source_target_pairs={{0,16},{8,24},{16,0},{24,8},{1,17},{9,25},{17,1},{25,9},{2,18},{10... | collective-permute-start | bytes 688136 | tf_op jit(solution)/shard_map/ppermute | solution.py:244
  29.8 2.2 %collective-permute-start.1 = (bf16[896,128]{1,0:T(8,128)(2,1)S(1)}, bf16[896,128]{1,0:T(8,128)(2,1)S(1)}, u32[]{:S(2)}, u32[]{:S(2)}) collective-permute-start(bf16[896,128]{1,0:T(8,128)(2,1)S(1)} %all_gather.3.refs_0_), channel_id=1, source_target_pairs={{0,8},{8,16},{16,24},{24,0},{1,9},{9,17},{17,25},{25,1},{2,10},{10... | collective-permute-start | bytes 688136 | tf_op jit(solution)/shard_map/ppermute | solution.py:244
  32.0 4.3 %collective-permute-start.2 = (bf16[896,128]{1,0:T(8,128)(2,1)S(1)}, bf16[896,128]{1,0:T(8,128)(2,1)S(1)}, u32[]{:S(2)}, u32[]{:S(2)}) collective-permute-start(bf16[896,128]{1,0:T(8,128)(2,1)S(1)} %all_gather.3.refs_0_), channel_id=1, source_target_pairs={{0,24},{8,0},{16,8},{24,16},{1,25},{9,1},{17,9},{25,17},{2,26},{10... | collective-permute-start | bytes 688136 | tf_op jit(solution)/shard_map/ppermute | solution.py:244
  36.3 10.7 %collective-permute-start.3 = (bf16[8,64,256]{2,1,0:T(8,128)(2,1)S(1)}, bf16[8,64,256]{2,1,0:T(8,128)(2,1)S(1)}, u32[]{:S(2)}, u32[]{:S(2)}) collective-permute-start(bf16[8,64,256]{2,1,0:T(8,128)(2,1)S(1)} %all_to_all.10.refs_4_), channel_id=1, source_target_pairs={{0,2},{2,4},{4,6},{6,256},{256,258},{258,260},{260,262},{262,0},{1... | collective-permute-start | bytes 786440 | tf_op jit(solution)/shard_map/ppermute | solution.py:240
  47.0 0.0 collective-permute-done.7
  47.0 2.2 %collective-permute-start.8 = (bf16[8,64,256]{2,1,0:T(8,128)(2,1)S(1)}, bf16[8,64,256]{2,1,0:T(8,128)(2,1)S(1)}, u32[]{:S(2)}, u32[]{:S(2)}) collective-permute-start(bf16[8,64,256]{2,1,0:T(8,128)(2,1)S(1)} %collective-permute-done.7), channel_id=1, source_target_pairs={{0,2},{2,4},{4,6},{6,256},{256,258},{258,260},{260,262},{262,0},{1... | collective-permute-start | bytes 786440 | tf_op jit(solution)/shard_map/ppermute | solution.py:240
  49.2 0.0 collective-permute-done.1.refs_2_
  49.2 0.0 collective-permute-done.2.refs_3_
  49.2 2.2 %shard_map.37.refs_5_ = f32[3584,256]{1,0:T(8,128)S(1)} custom-call(bf16[896,128]{1,0:T(8,128)(2,1)S(1)} %all_gather.3.refs_0_, bf16[896,128]{1,0:T(8,128)(2,1)S(1)} %collective-permute-done.refs_1_, bf16[896,128]{1,0:T(8,128)(2,1)S(1)} %collective-permute-done.1.refs_2_, bf16[896,128]{1,0:T(8,128)(2,1)S(1)} %collective-permute-done.2.refs_3_, ...), custom_call_target="tpu_custom_call" | custom-call | flops 1879048192 | bytes 1048576 | tf_op jit(solution)/shard_map/pallas_call | solution.py:272
  51.4 0.0 collective-permute-done.3.refs_4_.refs_5_
  51.4 3.9 %collective-permute-start.4 = (bf16[8,64,256]{2,1,0:T(8,128)(2,1)S(1)}, bf16[8,64,256]{2,1,0:T(8,128)(2,1)S(1)}, u32[]{:S(2)}, u32[]{:S(2)}) collective-permute-start(bf16[8,64,256]{2,1,0:T(8,128)(2,1)S(1)} %collective-permute-done.3.refs_4_.refs_5_), channel_id=1, source_target_pairs={{0,2},{2,4},{4,6},{6,256},{256,258},{258,260},{260,262},{262,0},{1... | collective-permute-start | bytes 786440 | tf_op jit(solution)/shard_map/ppermute | solution.py:240
  55.3 2.2 %shard_map.38.refs_5_ = f32[3584,256]{1,0:T(8,128)S(1)} custom-call(bf16[896,128]{1,0:T(8,128)(2,1)S(1)} %all_gather.3.refs_0_, bf16[896,128]{1,0:T(8,128)(2,1)S(1)} %collective-permute-done.refs_1_, bf16[896,128]{1,0:T(8,128)(2,1)S(1)} %collective-permute-done.1.refs_2_, ...), custom_call_target="tpu_custom_call", output_to_operand_aliasing={{}: (5, {})} | custom-call | flops 1879048192 | bytes 1048576 | tf_op jit(solution)/shard_map/pallas_call | solution.py:272
  57.5 0.0 collective-permute-done.8.refs_4_.refs_9_
  57.5 1.9 %collective-permute-start.9 = (bf16[8,64,256]{2,1,0:T(8,128)(2,1)S(1)}, bf16[8,64,256]{2,1,0:T(8,128)(2,1)S(1)}, u32[]{:S(2)}, u32[]{:S(2)}) collective-permute-start(bf16[8,64,256]{2,1,0:T(8,128)(2,1)S(1)} %collective-permute-done.8.refs_4_.refs_9_), channel_id=1, source_target_pairs={{0,2},{2,4},{4,6},{6,256},{256,258},{258,260},{260,262},{262,0},{1... | collective-permute-start | bytes 786440 | tf_op jit(solution)/shard_map/ppermute | solution.py:240
  59.4 2.2 %shard_map.39.refs_5_ = f32[3584,256]{1,0:T(8,128)S(1)} custom-call(bf16[896,128]{1,0:T(8,128)(2,1)S(1)} %all_gather.3.refs_0_, bf16[896,128]{1,0:T(8,128)(2,1)S(1)} %collective-permute-done.refs_1_, bf16[896,128]{1,0:T(8,128)(2,1)S(1)} %collective-permute-done.1.refs_2_, ...), custom_call_target="tpu_custom_call", output_to_operand_aliasing={{}: (5, {})} | custom-call | flops 1879048192 | bytes 1048576 | tf_op jit(solution)/shard_map/pallas_call | solution.py:272
  61.7 1.9 %collective-permute-start.5 = (bf16[8,64,256]{2,1,0:T(8,128)(2,1)S(1)}, bf16[8,64,256]{2,1,0:T(8,128)(2,1)S(1)}, u32[]{:S(2)}, u32[]{:S(2)}) collective-permute-start(bf16[8,64,256]{2,1,0:T(8,128)(2,1)S(1)} %collective-permute-done.4.refs_4_.refs_6_), channel_id=1, source_target_pairs={{0,2},{2,4},{4,6},{6,256},{256,258},{258,260},{260,262},{262,0},{1... | collective-permute-start | bytes 786440 | tf_op jit(solution)/shard_map/ppermute | solution.py:240
  63.6 2.2 %shard_map.40.refs_5_ = f32[3584,256]{1,0:T(8,128)S(1)} custom-call(bf16[896,128]{1,0:T(8,128)(2,1)S(1)} %all_gather.3.refs_0_, bf16[896,128]{1,0:T(8,128)(2,1)S(1)} %collective-permute-done.refs_1_, bf16[896,128]{1,0:T(8,128)(2,1)S(1)} %collective-permute-done.1.refs_2_, ...), custom_call_target="tpu_custom_call", output_to_operand_aliasing={{}: (5, {})} | custom-call | flops 1879048192 | bytes 1048576 | tf_op jit(solution)/shard_map/pallas_call | solution.py:272
  65.8 0.0 collective-permute-done.9.refs_4_.refs_10_
  65.8 1.9 %collective-permute-start.10 = (bf16[8,64,256]{2,1,0:T(8,128)(2,1)S(1)}, bf16[8,64,256]{2,1,0:T(8,128)(2,1)S(1)}, u32[]{:S(2)}, u32[]{:S(2)}) collective-permute-start(bf16[8,64,256]{2,1,0:T(8,128)(2,1)S(1)} %collective-permute-done.9.refs_4_.refs_10_), channel_id=1, source_target_pairs={{0,2},{2,4},{4,6},{6,256},{256,258},{258,260},{260,262},{262,0},{1... | collective-permute-start | bytes 786440 | tf_op jit(solution)/shard_map/ppermute | solution.py:240
  67.8 2.4 %shard_map.41.refs_5_ = f32[3584,256]{1,0:T(8,128)S(1)} custom-call(bf16[896,128]{1,0:T(8,128)(2,1)S(1)} %all_gather.3.refs_0_, bf16[896,128]{1,0:T(8,128)(2,1)S(1)} %collective-permute-done.refs_1_, bf16[896,128]{1,0:T(8,128)(2,1)S(1)} %collective-permute-done.1.refs_2_, ...), custom_call_target="tpu_custom_call", output_to_operand_aliasing={{}: (5, {})} | custom-call | flops 1879048192 | bytes 1048576 | tf_op jit(solution)/shard_map/pallas_call | solution.py:272
  70.2 2.7 %collective-permute-start.6 = (bf16[8,64,256]{2,1,0:T(8,128)(2,1)S(1)}, bf16[8,64,256]{2,1,0:T(8,128)(2,1)S(1)}, u32[]{:S(2)}, u32[]{:S(2)}) collective-permute-start(bf16[8,64,256]{2,1,0:T(8,128)(2,1)S(1)} %collective-permute-done.5.refs_4_.refs_7_), channel_id=1, source_target_pairs={{0,2},{2,4},{4,6},{6,256},{256,258},{258,260},{260,262},{262,0},{1... | collective-permute-start | bytes 786440 | tf_op jit(solution)/shard_map/ppermute | solution.py:240
  72.9 2.2 %shard_map.42.refs_5_ = f32[3584,256]{1,0:T(8,128)S(1)} custom-call(bf16[896,128]{1,0:T(8,128)(2,1)S(1)} %all_gather.3.refs_0_, bf16[896,128]{1,0:T(8,128)(2,1)S(1)} %collective-permute-done.refs_1_, bf16[896,128]{1,0:T(8,128)(2,1)S(1)} %collective-permute-done.1.refs_2_, ...), custom_call_target="tpu_custom_call", output_to_operand_aliasing={{}: (5, {})} | custom-call | flops 1879048192 | bytes 1048576 | tf_op jit(solution)/shard_map/pallas_call | solution.py:272
  75.1 0.0 collective-permute-done.10.refs_4_.refs_11_
  75.1 2.2 %shard_map.43.refs_12_ = f32[3584,256]{1,0:T(8,128)S(1)} custom-call(bf16[896,128]{1,0:T(8,128)(2,1)S(1)} %all_gather.3.refs_0_, bf16[896,128]{1,0:T(8,128)(2,1)S(1)} %collective-permute-done.refs_1_, bf16[896,128]{1,0:T(8,128)(2,1)S(1)} %collective-permute-done.1.refs_2_, ...), custom_call_target="tpu_custom_call", output_to_operand_aliasing={{}: (5, {})} | custom-call | flops 1879048192 | bytes 1048576 | tf_op jit(solution)/shard_map/pallas_call | solution.py:272
  77.3 0.0 copy-start
  77.3 1.0 %close.1 = bf16[8,480,128]{2,1,0:T(8,128)(2,1)S(1)} custom-call(bf16[896,128]{1,0:T(8,128)(2,1)S(1)} %all_gather.3.refs_0_, bf16[896,128]{1,0:T(8,128)(2,1)S(1)} %collective-permute-done.refs_1_, bf16[896,128]{1,0:T(8,128)(2,1)S(1)} %collective-permute-done.1.refs_2_, bf16[896,128]{1,0:T(8,128)(2,1)S(1)} %collective-permute-done.2.refs_3_, ...), custom_call_target="tpu_custom_call" | custom-call | flops 1879048192 | bytes 1048576 | tf_op jit(solution)/shard_map/close/pallas_call | solution.py:282
  78.4 20.3 %all_to_all.11.got_ref = bf16[8,480,128]{2,1,0:T(8,128)(2,1)S(1)} all-to-all(bf16[8,480,128]{2,1,0:T(8,128)(2,1)S(1)} %close.1), channel_id=1, replica_groups=mesh['zh'=2,'y'=8,'x'=4,'zl'=4,'c'=2] {'x','c'}, dimensions={0} | all-to-all | bytes 1966080 | tf_op jit(solution)/shard_map/all_to_all | solution.py:292
  98.7 1.9 %combine.1 = bf16[448,128]{1,0:T(8,128)(2,1)} custom-call(bf16[448,128]{1,0:T(8,128)(2,1)S(1)} %bitcast.3, bf16[8,480,128]{2,1,0:T(8,128)(2,1)S(1)} %all_to_all.11.got_ref), custom_call_target="tpu_custom_call" | custom-call | tf_op jit(solution)/shard_map/combine/pallas_call | solution.py:293
  (6 shorter events, 0.0 us)
Async XLA Ops:
  17.7 29.2 %collective-permute-start.7 = (bf16[8,64,256]{2,1,0:T(8,128)(2,1)S(1)}, bf16[8,64,256]{2,1,0:T(8,128)(2,1)S(1)}, u32[]{:S(2)}, u32[]{:S(2)}) collective-permute-start(bf16[8,64,256]{2,1,0:T(8,128)(2,1)S(1)} %all_to_all.10.refs_4_), channel_id=1, source_target_pairs={{0,1},{1,0},{2,3},{3,2},{4,5},{5,4},{6,7},{7,6},{8,9},{9,8},{10,11... | collective-permute-start | bytes 786440 | tf_op jit(solution)/shard_map/ppermute | solution.py:264
  25.1 24.0 %collective-permute-start = (bf16[896,128]{1,0:T(8,128)(2,1)S(1)}, bf16[896,128]{1,0:T(8,128)(2,1)S(1)}, u32[]{:S(2)}, u32[]{:S(2)}) collective-permute-start(bf16[896,128]{1,0:T(8,128)(2,1)S(1)} %all_gather.3.refs_0_), channel_id=1, source_target_pairs={{0,16},{8,24},{16,0},{24,8},{1,17},{9,25},{17,1},{25,9},{2,18},{10... | collective-permute-start | bytes 688136 | tf_op jit(solution)/shard_map/ppermute | solution.py:244
  29.8 19.4 %collective-permute-start.1 = (bf16[896,128]{1,0:T(8,128)(2,1)S(1)}, bf16[896,128]{1,0:T(8,128)(2,1)S(1)}, u32[]{:S(2)}, u32[]{:S(2)}) collective-permute-start(bf16[896,128]{1,0:T(8,128)(2,1)S(1)} %all_gather.3.refs_0_), channel_id=1, source_target_pairs={{0,8},{8,16},{16,24},{24,0},{1,9},{9,17},{17,25},{25,1},{2,10},{10... | collective-permute-start | bytes 688136 | tf_op jit(solution)/shard_map/ppermute | solution.py:244
  32.0 17.2 %collective-permute-start.2 = (bf16[896,128]{1,0:T(8,128)(2,1)S(1)}, bf16[896,128]{1,0:T(8,128)(2,1)S(1)}, u32[]{:S(2)}, u32[]{:S(2)}) collective-permute-start(bf16[896,128]{1,0:T(8,128)(2,1)S(1)} %all_gather.3.refs_0_), channel_id=1, source_target_pairs={{0,24},{8,0},{16,8},{24,16},{1,25},{9,1},{17,9},{25,17},{2,26},{10... | collective-permute-start | bytes 688136 | tf_op jit(solution)/shard_map/ppermute | solution.py:244
  36.3 15.1 %collective-permute-start.3 = (bf16[8,64,256]{2,1,0:T(8,128)(2,1)S(1)}, bf16[8,64,256]{2,1,0:T(8,128)(2,1)S(1)}, u32[]{:S(2)}, u32[]{:S(2)}) collective-permute-start(bf16[8,64,256]{2,1,0:T(8,128)(2,1)S(1)} %all_to_all.10.refs_4_), channel_id=1, source_target_pairs={{0,2},{2,4},{4,6},{6,256},{256,258},{258,260},{260,262},{262,0},{1... | collective-permute-start | bytes 786440 | tf_op jit(solution)/shard_map/ppermute | solution.py:240
  47.0 10.5 %collective-permute-start.8 = (bf16[8,64,256]{2,1,0:T(8,128)(2,1)S(1)}, bf16[8,64,256]{2,1,0:T(8,128)(2,1)S(1)}, u32[]{:S(2)}, u32[]{:S(2)}) collective-permute-start(bf16[8,64,256]{2,1,0:T(8,128)(2,1)S(1)} %collective-permute-done.7), channel_id=1, source_target_pairs={{0,2},{2,4},{4,6},{6,256},{256,258},{258,260},{260,262},{262,0},{1... | collective-permute-start | bytes 786440 | tf_op jit(solution)/shard_map/ppermute | solution.py:240
  51.4 10.2 %collective-permute-start.4 = (bf16[8,64,256]{2,1,0:T(8,128)(2,1)S(1)}, bf16[8,64,256]{2,1,0:T(8,128)(2,1)S(1)}, u32[]{:S(2)}, u32[]{:S(2)}) collective-permute-start(bf16[8,64,256]{2,1,0:T(8,128)(2,1)S(1)} %collective-permute-done.3.refs_4_.refs_5_), channel_id=1, source_target_pairs={{0,2},{2,4},{4,6},{6,256},{256,258},{258,260},{260,262},{262,0},{1... | collective-permute-start | bytes 786440 | tf_op jit(solution)/shard_map/ppermute | solution.py:240
  57.5 8.3 %collective-permute-start.9 = (bf16[8,64,256]{2,1,0:T(8,128)(2,1)S(1)}, bf16[8,64,256]{2,1,0:T(8,128)(2,1)S(1)}, u32[]{:S(2)}, u32[]{:S(2)}) collective-permute-start(bf16[8,64,256]{2,1,0:T(8,128)(2,1)S(1)} %collective-permute-done.8.refs_4_.refs_9_), channel_id=1, source_target_pairs={{0,2},{2,4},{4,6},{6,256},{256,258},{258,260},{260,262},{262,0},{1... | collective-permute-start | bytes 786440 | tf_op jit(solution)/shard_map/ppermute | solution.py:240
  61.7 8.5 %collective-permute-start.5 = (bf16[8,64,256]{2,1,0:T(8,128)(2,1)S(1)}, bf16[8,64,256]{2,1,0:T(8,128)(2,1)S(1)}, u32[]{:S(2)}, u32[]{:S(2)}) collective-permute-start(bf16[8,64,256]{2,1,0:T(8,128)(2,1)S(1)} %collective-permute-done.4.refs_4_.refs_6_), channel_id=1, source_target_pairs={{0,2},{2,4},{4,6},{6,256},{256,258},{258,260},{260,262},{262,0},{1... | collective-permute-start | bytes 786440 | tf_op jit(solution)/shard_map/ppermute | solution.py:240
  65.8 9.3 %collective-permute-start.10 = (bf16[8,64,256]{2,1,0:T(8,128)(2,1)S(1)}, bf16[8,64,256]{2,1,0:T(8,128)(2,1)S(1)}, u32[]{:S(2)}, u32[]{:S(2)}) collective-permute-start(bf16[8,64,256]{2,1,0:T(8,128)(2,1)S(1)} %collective-permute-done.9.refs_4_.refs_10_), channel_id=1, source_target_pairs={{0,2},{2,4},{4,6},{6,256},{256,258},{258,260},{260,262},{262,0},{1... | collective-permute-start | bytes 786440 | tf_op jit(solution)/shard_map/ppermute | solution.py:240
  70.2 7.2 %collective-permute-start.6 = (bf16[8,64,256]{2,1,0:T(8,128)(2,1)S(1)}, bf16[8,64,256]{2,1,0:T(8,128)(2,1)S(1)}, u32[]{:S(2)}, u32[]{:S(2)}) collective-permute-start(bf16[8,64,256]{2,1,0:T(8,128)(2,1)S(1)} %collective-permute-done.5.refs_4_.refs_7_), channel_id=1, source_target_pairs={{0,2},{2,4},{4,6},{6,256},{256,258},{258,260},{260,262},{262,0},{1... | collective-permute-start | bytes 786440 | tf_op jit(solution)/shard_map/ppermute | solution.py:240
  77.3 21.3 %copy-start = (bf16[7,64,128]{2,1,0:T(8,128)(2,1)S(1)}, bf16[7,64,128]{2,1,0:T(8,128)(2,1)}, u32[]{:S(2)}) copy-start(bf16[7,64,128]{2,1,0:T(8,128)(2,1)} %param.3) | copy-start | bytes 344068
